TPU v7x, 32 devices: a whole 2x2x4 slice. The times are simulated.
32 devices in a mesh: dp: 2 (over x), tm: 4 (over z), mp: 4 (over y, core).
Axes of the slice: x: 2, y: 2, z: 4, core: 2. Of those that a mesh axis runs over, the one named last changes fastest.
Arguments:
- features: bfloat16 [32, 576, 1024], P(('dp', 'tm'), 'mp'), parts along dimension 0, may hold values from -6 to 6
- queries: bfloat16 [2048, 1024], P(('dp', 'tm')), parts along dimension 0, may hold values from -6 to 6
- anchor_frame: int32 [2048], P(('dp', 'tm')), parts along dimension 0, may hold values from 0 to 15, as said below
- anchor_patch: int32 [2048], P(('dp', 'tm')), parts along dimension 0, may hold values from 0 to 575
- time_offset: float32 [2048, 8, 4], P(('dp', 'tm')), parts along dimension 0, may hold values from -1.99 to 1.99
- space_offset: float32 [2, 2048, 8, 4], P(None, ('dp', 'tm')), parts along dimension 1, may hold values from -3 to 3
- value_weight: bfloat16 [1024, 1024], replicated, may hold values from -0.1875 to 0.1875
- point_weight: bfloat16 [1024, 32], replicated, may hold values from -0.1875 to 0.1875
- point_bias: float32 [32], replicated, may hold values from -6 to 260
- output_weight: bfloat16 [1024, 1024], P('mp'), may hold values from -0.1875 to 0.1875
- project_weight: bfloat16 [1024, 3584], P(None, 'mp'), may hold values from -2 to 2
- norm_gain: float32 [3584], P('mp'), may hold values from 0.1 to 1.9
- query_weight: bfloat16 [3584, 3072], P(None, 'mp'), may hold values from -0.09375 to 0.09375
- query_bias: float32 [3072], P('mp'), may hold values from -6 to 40
- cache_weight: bfloat16 [3584, 1024], P(None, 'mp'), may hold values from -0.09375 to 0.09375
- cache_bias: float32 [1024], P('mp'), may hold values from -6 to 40
Outputs:
- attention: bfloat16 [2048, 3072], P(('dp', 'tm'), 'mp'), parts along dimension 0
- key_value: bfloat16 [2048, 1024], P(('dp', 'tm'), 'mp'), parts along dimension 0
There are 2 independent parts, one for each index of `dp`. A program takes and returns all parts, laid end to end along the dimension named above; an argument that names none is the same for every part. Nothing has to cross between parts.
Inputs may be any that keep to these rules, and one draw needn't show every extreme that they name: `anchor_frame`: the anchor frame of query q lies among the 4 frames that begin at (q // 256) * 4.
All inputs are finite; a program needn't handle non-finite values.
Results may differ from a plain program's by a relative error of at most 0.04.
Values may be sent and summed in bfloat16 or wider, within the bound.
A program may use at most 64 MiB of HBM per device.

v0:
```python
import functools

import jax
import jax.numpy as jnp
from jax import lax
from jax.experimental import pallas as pl
from jax.experimental.pallas import tpu as pltpu
from jax.sharding import PartitionSpec as P

AH = 8
POINTS = 4
GRID = 24
KVH = 4
HD = 128
GROUP = 7

rope_base = 1000000.0
epsilon = 1e-06
masked = -1e30
MESH = pl.DeviceIdType.MESH
BF = jnp.bfloat16
F32 = jnp.float32


def remote(src, dst, send, recv, device):
    return pltpu.make_async_remote_copy(
        src_ref=src, dst_ref=dst, send_sem=send, recv_sem=recv, device_id=device, device_id_type=MESH
    )


class Gather:
    def __init__(self, slot_ref, own, sems, groups, me):
        self.chips = groups // 2
        self.chip, self.core = me // 2, me % 2
        self.me, self.partner = me, me + 1 - 2 * (me % 2)
        cs, cr, ps, pr = sems
        self.cross = [None] + [
            remote(
                own,
                slot_ref(me),
                cs(d),
                cr(d),
                {"mp": (self.chip + d) % self.chips * 2 + self.core},
            )
            for d in range(1, self.chips)
        ]
        self.near = [remote(own, slot_ref(me), ps(0), pr(0), {"mp": self.partner})]
        for d in range(1, self.chips):
            slot = slot_ref(self.slot(d, self.core))
            self.near.append(remote(slot, slot, ps(d), pr(d), {"mp": self.partner}))

    def slot(self, d, core):
        return (self.chip + self.chips - d) % self.chips * 2 + core

    def start(self):
        for copy in self.cross[1:]:
            copy.start()
        self.near[0].start()

    def arrivals(self):
        self.near[0].wait_recv()
        yield self.partner
        for d in range(1, self.chips):
            self.cross[d].wait_recv()
            self.near[d].start()
            yield self.slot(d, self.core)
            self.near[d].wait_recv()
            yield self.slot(d, 1 - self.core)

    def drain(self):
        for copy in self.cross[1:] + self.near:
            copy.wait_send()


def kernel(
    groups,
    spans,
    frames,
    features,
    queries,
    coords,
    cosine,
    sine,
    gain,
    query_bias,
    cache_bias,
    value_hbm,
    output_hbm,
    project_hbm,
    query_hbm,
    cache_hbm,
    attention,
    key_value,
    vw,
    wo,
    wp,
    wq,
    wc,
    halo,
    own_values,
    halo_values,
    corner,
    partial,
    rs_send,
    rs_recv,
    ab,
    vx,
    ssq,
    q_acc,
    kv_acc,
    qs,
    kv,
    peak,
    denom,
    numer,
    load_sem,
    halo_send,
    halo_recv,
    rs_ss,
    rs_rs,
    sq_ss,
    sq_rs,
    z_ss,
    z_rs,
    ag_sem,
):
    me = lax.axis_index("mp")
    t = lax.axis_index("tm")
    cells, width = features.shape
    rows = queries.shape[0]
    half = 2 * (cells // frames)
    lines = cells // frames // GRID
    piece = rows // groups
    model = wp.shape[1]
    q_heads = qs.shape[0]
    ch = kv.shape[3] // HD

    loads = [
        pltpu.make_async_copy(src, dst, load_sem.at[i])
        for i, (src, dst) in enumerate(
            [
                (value_hbm, vw),
                (output_hbm, wo.at[me]),
                (project_hbm, wp),
                (cache_hbm, wc),
                (query_hbm, wq),
            ]
        )
    ]
    for load in loads:
        load.start()

    barrier = pltpu.get_barrier_semaphore()
    for d in range(1, groups):
        pl.semaphore_signal(barrier, inc=1, device_id={"mp": (me + d) % groups}, device_id_type=MESH)
    for d in range(1, spans):
        pl.semaphore_signal(barrier, inc=1, device_id={"tm": (t + d) % spans}, device_id_type=MESH)
    pl.semaphore_wait(barrier, groups + spans - 2)

    low, high = halo.at[pl.ds(0, half)], halo.at[pl.ds(half, half)]
    up = remote(
        features.at[pl.ds(cells - half, half)], low, halo_send.at[0], halo_recv.at[0], {"tm": (t + 1) % spans}
    )
    down = remote(
        features.at[pl.ds(0, half)],
        high,
        halo_send.at[1],
        halo_recv.at[1],
        {"tm": (t + spans - 1) % spans},
    )

    @pl.when(t < spans - 1)
    def _():
        up.start()

    @pl.when(t > 0)
    def _():
        down.start()

    @pl.when(t == 0)
    def _():
        halo[pl.ds(0, half), :] = jnp.zeros((half, width), BF)

    @pl.when(t == spans - 1)
    def _():
        halo[pl.ds(half, half), :] = jnp.zeros((half, width), BF)

    def gather_sems(index):
        return [functools.partial(lambda k, d: ag_sem.at[index, k, d], k) for k in range(4)]

    wo_gather = Gather(lambda s: wo.at[s], output_hbm, gather_sems(0), groups, me)
    wo_gather.start()

    loads[0].wait()

    def project_values(source, target):
        @pl.loop(0, width // 256)
        def _(c):
            cols = pl.ds(pl.multiple_of(c * 256, 256), 256)
            target[:, cols] = jnp.dot(
                source[...], vw[:, cols], preferred_element_type=F32
            ).astype(BF)

    line_index = lax.broadcasted_iota(jnp.int32, (GRID, rows), 0).astype(F32)
    first_line = (me * lines).astype(F32)
    first_frame = (t * frames).astype(F32)

    def hat(position, cell):
        return jnp.maximum(1.0 - jnp.abs(position - cell), 0.0)

    def sample(values, offsets, head):
        info = coords[head]
        columns = [hat(info[8 + k : 9 + k], line_index) for k in range(POINTS)]
        for f, offset in enumerate(offsets):
            timed = info[12:16] * hat(info[0:4], first_frame + offset)
            for line in range(lines):
                share = timed * hat(info[4:8], first_line + line)
                total = share[0:1] * columns[0]
                for k in range(1, POINTS):
                    total = total + share[k : k + 1] * columns[k]
                corner[pl.ds((f * lines + line) * GRID, GRID), :] = total
        cols = pl.ds(pl.multiple_of(head * HD, HD), HD)
        return lax.dot_general(
            corner[pl.ds(0, values.shape[0]), :].astype(BF),
            values[:, cols],
            (((0,), (0,)), ((), ())),
            preferred_element_type=F32,
        )

    project_values(features, own_values)

    @pl.loop(0, AH)
    def _(head):
        cols = pl.ds(pl.multiple_of(head * HD, HD), HD)
        partial[:, cols] = sample(own_values, range(frames), head)

    @pl.when(t > 0)
    def _():
        up.wait_recv()

    @pl.when(t < spans - 1)
    def _():
        down.wait_recv()

    project_values(halo, halo_values)

    @pl.loop(0, AH)
    def _(head):
        cols = pl.ds(pl.multiple_of(head * HD, HD), HD)
        total = partial[:, cols] + sample(halo_values, (-2, -1, frames, frames + 1), head)
        rs_send[:, :, cols] = total.reshape(groups, piece, HD).astype(BF)

    rs = []
    for d in range(1, groups):
        peer = (me + d) % groups
        copy = remote(rs_send.at[peer], rs_recv.at[d], rs_ss.at[d], rs_rs.at[d], {"mp": peer})
        copy.start()
        rs.append(copy)

    loads[1].wait()
    for _ in wo_gather.arrivals():
        pass

    total = rs_send[me].astype(F32)
    for d in range(1, groups):
        rs[d - 1].wait_recv()
        total = total + rs_recv[d].astype(F32)
    mixed = jnp.dot(total.astype(BF), wo[...].reshape(width, width), preferred_element_type=F32)
    own_rows = pl.ds(pl.multiple_of(me * piece, piece), piece)
    ab[me] = (queries[own_rows, :].astype(F32) + mixed).astype(BF)
    ab_gather = Gather(lambda s: ab.at[s], ab.at[me], gather_sems(1), groups, me)
    ab_gather.start()
    loads[2].wait()
    for _ in ab_gather.arrivals():
        pass

    visual = jnp.dot(ab[...].reshape(rows, width), wp[...], preferred_element_type=F32)
    vx[me] = (visual * gain[...]).astype(BF)
    vx_gather = Gather(lambda s: vx.at[s], vx.at[me], gather_sems(2), groups, me)
    vx_gather.start()
    squares = jnp.broadcast_to(jnp.sum(visual * visual, axis=1, keepdims=True), (rows, HD)).T
    ssq[0] = squares[0:8]
    sq = []
    for d in range(1, groups):
        copy = remote(
            ssq.at[0], ssq.at[d], sq_ss.at[d], sq_rs.at[d], {"mp": (me + d) % groups}
        )
        copy.start()
        sq.append(copy)

    q_width = wq.shape[1]
    tile = 256 if q_width % 256 == 0 else 128

    def slot_rows(slot):
        return pl.ds(pl.multiple_of(slot * model, 64), model)

    def add_cache(slot, first):
        term = jnp.dot(vx[slot], wc[slot_rows(slot), :], preferred_element_type=F32)
        kv_acc[...] = term if first else kv_acc[...] + term

    def add_query(slot, first):
        @pl.loop(0, q_width // tile)
        def _(c):
            cols = pl.ds(pl.multiple_of(c * tile, tile), tile)
            term = jnp.dot(vx[slot], wq[slot_rows(slot), cols], preferred_element_type=F32)
            q_acc[:, cols] = term if first else q_acc[:, cols] + term

    loads[3].wait()
    loads[4].wait()
    add_cache(me, True)
    add_query(me, True)
    for order, slot in enumerate(vx_gather.arrivals()):
        add_cache(slot, False)
        if order < groups - 2:
            add_query(slot, False)
        last = slot

    square_sum = ssq[0]
    for d in range(1, groups):
        sq[d - 1].wait_recv()
        square_sum = square_sum + ssq[d]
    scale_row = lax.rsqrt(square_sum * (1.0 / (model * groups)) + epsilon)
    scale = jnp.broadcast_to(scale_row[0:1], (HD, rows)).T

    def turn(x, cos, sin):
        return x * cos + pltpu.roll(x, HD // 2, 1) * sin

    for i in range(ch):
        is_key = me * ch + i < KVH
        cols = slice(i * HD, (i + 1) * HD)
        state = kv_acc[:, cols] * scale + cache_bias[:, cols]
        cos = jnp.where(is_key, cosine[...], 1.0)
        sin = jnp.where(is_key, sine[...], 0.0)
        state = turn(state, cos, sin).astype(BF)
        kv[t, me, :, cols] = state
        key_value[:, cols] = state

    mine = kv.at[t, me]
    z_copies = []
    for d in range(1, spans):
        z_copies.append(remote(mine, mine, z_ss.at[d], z_rs.at[d], {"tm": (t + d) % spans}))

        @pl.when(t + d < spans)
        def _(d=d):
            z_copies[d - 1].start()

    def block_gather(d):
        j = lax.rem(t + spans - d, spans)
        return j, Gather(lambda s: kv.at[j, s], kv.at[j, me], gather_sems(3 + d), groups, me)

    own_gather = block_gather(0)
    own_gather[1].start()
    add_query(last, False)
    for i in range(q_heads):
        cols = slice(i * HD, (i + 1) * HD)
        state = q_acc[:, cols] * scale + query_bias[:, cols]
        qs[i] = turn(state, cosine[...], sine[...]).astype(BF)

    def attend(j, diagonal):
        @pl.loop(0, q_heads)
        def _(i):
            g = (me * q_heads + i) // GROUP
            k_cols = pl.ds(pl.multiple_of(lax.rem(g, ch) * HD, HD), HD)
            keys = kv[j, g // ch, :, k_cols]
            values = kv[j, (KVH + g) // ch, :, pl.ds(pl.multiple_of(lax.rem(KVH + g, ch) * HD, HD), HD)]
            scores = lax.dot_general(
                qs[i], keys, (((1,), (1,)), ((), ())), preferred_element_type=F32
            ) * (HD ** -0.5)
            if diagonal:
                q_pos = lax.broadcasted_iota(jnp.int32, (rows, rows), 0)
                k_pos = lax.broadcasted_iota(jnp.int32, (rows, rows), 1)
                scores = jnp.where(k_pos <= q_pos, scores, masked)
            top = jnp.max(scores, axis=1, keepdims=True)
            if diagonal:
                new_peak = jnp.broadcast_to(top, (rows, HD))
            else:
                new_peak = jnp.maximum(peak[i], top)
            weights = jnp.exp(scores - new_peak[:, 0:1])
            added = jnp.sum(weights, axis=1, keepdims=True)
            product = jnp.dot(weights.astype(BF), values, preferred_element_type=F32)
            if diagonal:
                denom[i] = jnp.broadcast_to(added, (rows, HD))
                numer[i] = product
            else:
                rescale = jnp.exp(peak[i] - new_peak)
                denom[i] = denom[i] * rescale + added
                numer[i] = numer[i] * rescale + product
            peak[i] = new_peak

    for _ in own_gather[1].arrivals():
        pass
    attend(t, True)
    for d in range(1, spans):

        @pl.when(t >= d)
        def _(d=d):
            j, gather = block_gather(d)
            arrived = kv.at[j, me]
            remote(arrived, arrived, z_ss.at[d], z_rs.at[d], {"tm": t}).wait_recv()
            gather.start()
            for _ in gather.arrivals():
                pass
            attend(j, False)
            gather.drain()

    for i in range(q_heads):
        attention[:, i * HD : (i + 1) * HD] = (numer[i] / denom[i]).astype(BF)

    @pl.when(t < spans - 1)
    def _():
        up.wait_send()

    @pl.when(t > 0)
    def _():
        down.wait_send()

    for gather in (wo_gather, ab_gather, vx_gather, own_gather[1]):
        gather.drain()
    for copy in rs + sq:
        copy.wait_send()
    for d in range(1, spans):

        @pl.when(t + d < spans)
        def _(d=d):
            z_copies[d - 1].wait_send()


def local(
    features,
    queries,
    anchor_frame,
    anchor_patch,
    time_offset,
    space_offset,
    value_weight,
    point_weight,
    point_bias,
    output_weight,
    project_weight,
    norm_gain,
    query_weight,
    query_bias,
    cache_weight,
    cache_bias,
):
    groups = lax.axis_size("mp")
    spans = lax.axis_size("tm")
    frames_here, patches_here, width = features.shape
    cells = frames_here * patches_here
    rows = queries.shape[0]
    logits = jnp.dot(queries, point_weight, preferred_element_type=F32) + point_bias
    share = jax.nn.softmax(logits.reshape(rows, AH, POINTS), axis=-1)
    frame_pos = anchor_frame.astype(F32)[:, None, None] + time_offset
    row_pos = (anchor_patch // GRID).astype(F32)[:, None, None] + space_offset[0]
    column_pos = (anchor_patch % GRID).astype(F32)[:, None, None] + space_offset[1]
    coords = jnp.stack([frame_pos, row_pos, column_pos, share], axis=0)
    coords = coords.transpose(2, 0, 3, 1).reshape(AH, 4 * POINTS, rows)
    positions = lax.axis_index("tm") * rows + jnp.arange(rows, dtype=jnp.int32)
    frequency = rope_base ** (-2.0 * jnp.arange(HD // 2, dtype=F32) / HD)
    angles = positions.astype(F32)[:, None] * frequency[None, :]
    cosine = jnp.cos(angles)
    sine = jnp.sin(angles)
    cosine = jnp.concatenate([cosine, cosine], axis=1)
    sine = jnp.concatenate([-sine, sine], axis=1)
    model = project_weight.shape[1]
    q_width = query_weight.shape[1]
    c_width = cache_weight.shape[1]
    q_heads = q_width // HD
    piece = rows // groups
    chips = groups // 2
    vmem = pl.BlockSpec(memory_space=pltpu.VMEM)
    hbm = pl.BlockSpec(memory_space=pl.ANY)
    dma = pltpu.SemaphoreType.DMA
    V = pltpu.VMEM
    return tuple(
        pl.pallas_call(
            functools.partial(kernel, groups, spans, frames_here),
            out_shape=(
                jax.ShapeDtypeStruct((rows, q_width), BF),
                jax.ShapeDtypeStruct((rows, c_width), BF),
            ),
            in_specs=[vmem] * 8 + [hbm] * 5,
            out_specs=(vmem, vmem),
            scratch_shapes=[
                V((width, width), BF),
                V((groups, width // groups, width), BF),
                V((width, model), BF),
                V(query_weight.shape, BF),
                V(cache_weight.shape, BF),
                V((4 * patches_here, width), BF),
                V((cells, width), BF),
                V((4 * patches_here, width), BF),
                V((max(4, frames_here) * patches_here, rows), F32),
                V((rows, width), F32),
                V((groups, piece, width), BF),
                V((groups, piece, width), BF),
                V((groups, piece, width), BF),
                V((groups, rows, model), BF),
                V((groups, 8, rows), F32),
                V((rows, q_width), F32),
                V((rows, c_width), F32),
                V((q_heads, rows, HD), BF),
                V((spans, groups, rows, c_width), BF),
                V((q_heads, rows, HD), F32),
                V((q_heads, rows, HD), F32),
                V((q_heads, rows, HD), F32),
                dma((5,)),
                dma((2,)),
                dma((2,)),
                dma((groups,)),
                dma((groups,)),
                dma((groups,)),
                dma((groups,)),
                dma((spans,)),
                dma((spans,)),
                dma((3 + spans, 4, chips)),
            ],
            compiler_params=pltpu.CompilerParams(
                collective_id=0, has_side_effects=True, vmem_limit_bytes=60 * 1024 * 1024
            ),
        )(
            features.reshape(cells, width),
            queries,
            coords,
            cosine,
            sine,
            norm_gain[None],
            query_bias[None],
            cache_bias[None],
            value_weight,
            output_weight,
            project_weight,
            query_weight,
            cache_weight,
        )
    )


def solution(mesh):
    return jax.shard_map(
        local,
        mesh=mesh,
        in_specs=(
            P(("dp", "tm"), "mp", None),
            P(("dp", "tm"), None),
            P(("dp", "tm")),
            P(("dp", "tm")),
            P(("dp", "tm"), None, None),
            P(None, ("dp", "tm"), None, None),
            P(),
            P(),
            P(),
            P("mp", None),
            P(None, "mp"),
            P("mp"),
            P(None, "mp"),
            P("mp"),
            P(None, "mp"),
            P("mp"),
        ),
        out_specs=(P(("dp", "tm"), "mp"), P(("dp", "tm"), "mp")),
        check_vma=False,
    )
```

profile of v0, /device:TPU:27, one launch (start us, length us, event | category | flops | bytes accessed | tf_op | source)
XLA Modules:
  0.0 100.7 jit_solution(16767075607597906509)
XLA Ops:
  0.6 0.0 copy-start
  0.7 0.7 convert_element_type.16
  1.4 0.7 fusion.2
  2.1 1.3 %broadcast_in_dim.7.query_bias = f32[1,768]{1,0:T(1,128)} reshape(f32[768]{0:T(1024)} %param.29) | data formatting | bytes 6144 | tf_op jit(solution)/shard_map/broadcast_in_dim | solution.py:528
  3.3 1.3 %broadcast_in_dim.6.gain = f32[1,896]{1,0:T(1,128)} reshape(f32[896]{0:T(1024)} %param.27) | data formatting | bytes 7168 | tf_op jit(solution)/shard_map/broadcast_in_dim | solution.py:527
  4.6 0.8 add_bitcast_fusion
  5.4 0.0 copy-done
  5.4 1.3 %convolution_add_fusion = f32[256,32]{0,1:T(8,128)S(1)} fusion(bf16[256,1024]{1,0:T(8,128)(2,1)} %queries.1, bf16[1024,32]{0,1:T(8,128)(2,1)S(1)} %copy-done, f32[32]{0:T(128)} %param.24), kind=kOutput, calls=%fused_computation | convolution fusion | flops 16785408 | bytes 622720 | tf_op jit(solution)/shard_map/dot_general | solution.py:451
  6.8 0.8 slice_add_fusion.1
  7.7 0.7 reshape.50.coords
  8.4 0.5 fusion
  8.9 0.8 pad_maximum_fusion
  9.7 87.6 %shard_map.167 = (bf16[256,768]{1,0:T(8,128)(2,1)}, bf16[256,256]{1,0:T(8,128)(2,1)}) custom-call(bf16[576,1024]{1,0:T(8,128)(2,1)} %bitcast.12, bf16[256,1024]{1,0:T(8,128)(2,1)} %queries.1, f32[8,16,256]{2,1,0:T(8,128)} %reshape.50.coords, f32[256,128]{1,0:T(8,128)} %get-tuple-element.10.cosine, f32[256,128]{1,0:T(8,128)} %get-tuple-element.11.sine, ...), custom_call_target="tpu_custom_call" | custom-call | tf_op jit(solution)/shard_map/pallas_call | solution.py:476
  97.3 1.8 %copy.21 = bf16[256,768]{1,0:T(8,128)(2,1)} copy(bf16[256,768]{1,0:T(8,128)(2,1)} %get-tuple-element.14) | data formatting | bytes 786432
  99.1 1.6 %copy.22 = bf16[256,256]{1,0:T(8,128)(2,1)} copy(bf16[256,256]{1,0:T(8,128)(2,1)} %get-tuple-element.15) | data formatting | bytes 262144
  (8 shorter events, 0.1 us)
Async XLA Ops:
  0.6 4.7 %copy-start = (bf16[1024,32]{0,1:T(8,128)(2,1)S(1)}, bf16[1024,32]{0,1:T(8,128)(2,1)}, u32[]{:S(2)}) copy-start(bf16[1024,32]{0,1:T(8,128)(2,1)} %param.23) | copy-start | bytes 196612
where the time goes:
time: 101 us
  Pallas kernels  87.6 us (87%)
  local copies, waits for them, and re-layouts  6.64 us (7%)
  other arithmetic  4.42 us (4%)
  matrix products  1.31 us (1%)
    pallas_call x1, Pallas kernels, local(): pl.pallas_call(functools.partial(kernel, groups, spans, frames_here), out...  87.6 us
    unnamed x4, local copies, waits for them, and re-layouts  3.34 us

commit v1 on v0

v1 whole, which is shorter than its diff:
```python
import functools

import jax
import jax.numpy as jnp
import numpy as np
from jax import lax
from jax.experimental import pallas as pl
from jax.experimental.pallas import tpu as pltpu
from jax.sharding import PartitionSpec as P

AH = 8
POINTS = 4
GRID = 24
KVH = 4
HD = 128
GROUP = 7

rope_base = 1000000.0
epsilon = 1e-06
masked = -1e30
chunk_rows = 128
MESH = pl.DeviceIdType.MESH
BF = jnp.bfloat16
F32 = jnp.float32


def remote(src, dst, send, recv, device):
    return pltpu.make_async_remote_copy(
        src_ref=src, dst_ref=dst, send_sem=send, recv_sem=recv, device_id=device, device_id_type=MESH
    )


class Gather:
    def __init__(self, slot_ref, own, sems, groups, me):
        self.chips = groups // 2
        self.chip, self.core = me // 2, me % 2
        self.me, self.partner = me, me + 1 - 2 * (me % 2)
        cs, cr, ps, pr = sems
        self.cross = [None] + [
            remote(
                own,
                slot_ref(me),
                cs(d),
                cr(d),
                {"mp": (self.chip + d) % self.chips * 2 + self.core},
            )
            for d in range(1, self.chips)
        ]
        self.near = [remote(own, slot_ref(me), ps(0), pr(0), {"mp": self.partner})]
        for d in range(1, self.chips):
            slot = slot_ref(self.slot(d, self.core))
            self.near.append(remote(slot, slot, ps(d), pr(d), {"mp": self.partner}))

    def slot(self, d, core):
        return (self.chip + self.chips - d) % self.chips * 2 + core

    def start(self):
        for copy in self.cross[1:]:
            copy.start()
        self.near[0].start()

    def arrivals(self):
        self.near[0].wait_recv()
        yield self.partner
        for d in range(1, self.chips):
            self.cross[d].wait_recv()
            self.near[d].start()
            yield self.slot(d, self.core)
            self.near[d].wait_recv()
            yield self.slot(d, 1 - self.core)

    def drain(self):
        for copy in self.cross[1:] + self.near:
            copy.wait_send()


def shared_heads(groups, q_heads, ch):
    table = []
    for source in range(groups):
        for target in range(groups):
            wanted = {(target * q_heads + i) // GROUP for i in range(q_heads)}
            need = [h for h in range(ch) if (source * ch + h) % KVH in wanted]
            if target != source and need:
                table.append((source, target, need[0], need[-1] - need[0] + 1))
    return table


def flat(ref):
    return jnp.concatenate([ref[i : i + 1, :] for i in range(ref.shape[0])], axis=1)


def kernel(
    groups,
    spans,
    frames,
    chunks,
    features,
    queries_hbm,
    row_turn_hbm,
    anchor_frame,
    anchor_patch,
    time_offset,
    space_offset,
    point_weight,
    point_bias,
    span_turn,
    gain,
    query_bias,
    cache_bias,
    value_hbm,
    output_hbm,
    project_hbm,
    query_hbm,
    cache_hbm,
    attention,
    key_value,
    own_features,
    queries,
    row_turn,
    vw,
    wo,
    wp,
    wq,
    wc,
    halo,
    own_values,
    halo_values,
    logits,
    coords,
    cosine,
    sine,
    corner,
    partial,
    rs_send,
    rs_recv,
    ex,
    ab,
    vx,
    ssq,
    scale,
    q_acc,
    kv_acc,
    qs,
    kv,
    peak,
    denom,
    numer,
    load_sem,
    halo_ss,
    halo_rs,
    rs_ss,
    rs_rs,
    ex_ss,
    ex_rs,
    ab_ss,
    ab_rs,
    sq_ss,
    sq_rs,
    z_ss,
    z_rs,
    d_ss,
    d_rs,
    ag_sem,
):
    me = lax.axis_index("mp")
    t = lax.axis_index("tm")
    cells, width = features.shape
    rows = queries.shape[0]
    per_frame = cells // frames
    lines = per_frame // GRID
    model = wp.shape[1]
    q_width = wq.shape[1]
    q_heads = qs.shape[0]
    ch = kv.shape[3] // HD
    chips = groups // 2
    chip, core = me // 2, me % 2
    partner = me + 1 - 2 * core
    size = rows // chunks
    part = size // 2

    loads = [
        pltpu.make_async_copy(src, dst, load_sem.at[i])
        for i, (src, dst) in enumerate(
            [
                (queries_hbm, queries),
                (features, own_features),
                (value_hbm, vw),
                (output_hbm, wo.at[me]),
                (row_turn_hbm, row_turn),
                (project_hbm, wp),
                (cache_hbm, wc),
                (query_hbm, wq),
            ]
        )
    ]
    for load in loads:
        load.start()

    barrier = pltpu.get_barrier_semaphore()
    for d in range(1, groups):
        pl.semaphore_signal(barrier, inc=1, device_id={"mp": (me + d) % groups}, device_id_type=MESH)

    @pl.when(t < spans - 1)
    def _():
        pl.semaphore_signal(barrier, inc=1, device_id={"tm": (t + 1) % spans}, device_id_type=MESH)

    @pl.when(t > 0)
    def _():
        pl.semaphore_signal(barrier, inc=1, device_id={"tm": (t + spans - 1) % spans}, device_id_type=MESH)

    neighbours = jnp.where(t > 0, 1, 0) + jnp.where(t < spans - 1, 1, 0)
    pl.semaphore_wait(barrier, groups - 1 + neighbours)

    up, down = [], []
    for i in range(2):
        up.append(
            remote(
                features.at[pl.ds((frames - 1 - i) * per_frame, per_frame)],
                halo.at[pl.ds(2 * i * per_frame, per_frame)],
                halo_ss.at[0, i],
                halo_rs.at[0, i],
                {"tm": (t + 1) % spans},
            )
        )
        down.append(
            remote(
                features.at[pl.ds(i * per_frame, per_frame)],
                halo.at[pl.ds((2 * i + 1) * per_frame, per_frame)],
                halo_ss.at[1, i],
                halo_rs.at[1, i],
                {"tm": (t + spans - 1) % spans},
            )
        )

    @pl.when(t < spans - 1)
    def _():
        for copy in up:
            copy.start()

    @pl.when(t > 0)
    def _():
        for copy in down:
            copy.start()

    def gather_sems(index):
        return [functools.partial(lambda k, d: ag_sem.at[index, k, d], k) for k in range(4)]

    wo_gather = Gather(lambda s: wo.at[s], output_hbm, gather_sems(0), groups, me)
    wo_gather.start()

    @pl.when(t == 0)
    def _():
        for i in range(2):
            halo[pl.ds(2 * i * per_frame, per_frame), :] = jnp.zeros((per_frame, width), BF)

    @pl.when(t == spans - 1)
    def _():
        for i in range(2):
            halo[pl.ds((2 * i + 1) * per_frame, per_frame), :] = jnp.zeros((per_frame, width), BF)

    loads[0].wait()
    logits[...] = jnp.zeros((rows, HD), F32)
    logits[:, 0 : AH * POINTS] = (
        lax.dot_general(
            queries[...], point_weight[...], (((1,), (1,)), ((), ())), preferred_element_type=F32
        )
        + point_bias[...]
    )
    by_point = logits[...].T
    frame_at = anchor_frame[...].astype(F32)
    patch = anchor_patch[...].astype(F32)
    row_at = jnp.floor((patch + 0.5) * (1.0 / GRID))
    column_at = patch - row_at * GRID
    for h in range(AH):
        own = by_point[h * POINTS : (h + 1) * POINTS]
        own = jnp.exp(own - jnp.max(own, axis=0, keepdims=True))
        coords[h, 0:4, :] = time_offset[h] + frame_at
        coords[h, 4:8, :] = space_offset[0, h] + row_at
        coords[h, 8:12, :] = space_offset[1, h] + column_at
        coords[h, 12:16, :] = own / jnp.sum(own, axis=0, keepdims=True)

    loads[1].wait()
    loads[2].wait()

    def project_values(source, target):
        for c in range(width // 256):
            cols = slice(c * 256, (c + 1) * 256)
            target[:, cols] = jnp.dot(source[...], vw[:, cols], preferred_element_type=F32).astype(BF)

    line_index = lax.broadcasted_iota(jnp.int32, (GRID, rows), 0).astype(F32)
    first_line = (me * lines).astype(F32)
    first_frame = (t * frames).astype(F32)

    def hat(position, cell):
        return jnp.maximum(1.0 - jnp.abs(position - cell), 0.0)

    def sample(values, offsets, head):
        info = coords[head]
        columns = [hat(info[8 + k : 9 + k], line_index) for k in range(POINTS)]
        for f, offset in enumerate(offsets):
            timed = info[12:16] * hat(info[0:4], first_frame + offset)
            for line in range(lines):
                share = timed * hat(info[4:8], first_line + line)
                total = share[0:1] * columns[0]
                for k in range(1, POINTS):
                    total = total + share[k : k + 1] * columns[k]
                corner[pl.ds((f * lines + line) * GRID, GRID), :] = total
        cols = pl.ds(pl.multiple_of(head * HD, HD), HD)
        return lax.dot_general(
            corner[pl.ds(0, values.shape[0]), :].astype(BF),
            values[:, cols],
            (((0,), (0,)), ((), ())),
            preferred_element_type=F32,
        )

    project_values(own_features, own_values)


    @pl.loop(0, AH)
    def _(head):
        cols = pl.ds(pl.multiple_of(head * HD, HD), HD)
        partial[:, cols] = sample(own_values, range(frames), head)

    loads[4].wait()
    span_cos, span_sin = span_turn[0, pl.ds(t, 1), :], span_turn[1, pl.ds(t, 1), :]
    cosine[...] = span_cos * row_turn[0] - span_sin * row_turn[1]
    sine[...] = span_sin * row_turn[0] + span_cos * row_turn[1]

    for i in range(2):

        @pl.when(t > 0)
        def _(i=i):
            up[i].wait_recv()

        @pl.when(t < spans - 1)
        def _(i=i):
            down[i].wait_recv()

        both = pl.ds(2 * i * per_frame, 2 * per_frame)
        project_values(halo.at[both], halo_values)

        @pl.loop(0, AH)
        def _(head, i=i):
            cols = pl.ds(pl.multiple_of(head * HD, HD), HD)
            partial[:, cols] = partial[:, cols] + sample(halo_values, (-1 - i, frames + i), head)

        if i == 0:
            loads[3].wait()
            for _ in wo_gather.arrivals():
                pass


    def rows_of(k, which):
        return pl.ds(pl.multiple_of(k * size + which * part, part), part)

    rs = []
    for k in range(chunks):
        rs_send[k] = partial[rows_of(k, 1 - core), :].astype(BF)
        rs.append(remote(rs_send.at[k], rs_recv.at[k], rs_ss.at[k], rs_rs.at[k], {"mp": partner}))
        rs[k].start()
    exchange = []
    for k in range(chunks):
        rs[k].wait_recv()
        ex[chip, k] = (partial[rows_of(k, core), :] + rs_recv[k].astype(F32)).astype(BF)
        copies = []
        for d in range(1, chips):
            mine = ex.at[chip, k]
            copies.append(
                remote(mine, mine, ex_ss.at[k, d], ex_rs.at[k, d], {"mp": (chip + d) % chips * 2 + core})
            )
            copies[-1].start()
        exchange.append(copies)
    loads[5].wait()

    def chunk_slice(k):
        return slice(k * size, (k + 1) * size)

    vx_gathers, ab_copies, sq = [], [], []
    for k in range(chunks):
        for copy in exchange[k]:
            copy.wait_recv()
        total = ex[0, k].astype(F32)
        for c in range(1, chips):
            total = total + ex[c, k].astype(F32)
        mixed = jnp.dot(total.astype(BF), wo[...].reshape(width, width), preferred_element_type=F32)
        ab[k, core] = (queries[rows_of(k, core), :].astype(F32) + mixed).astype(BF)
        mine = ab.at[k, core]
        ab_copies.append(remote(mine, mine, ab_ss.at[k], ab_rs.at[k], {"mp": partner}))
        ab_copies[k].start()
        ab_copies[k].wait_recv()
        visual = jnp.dot(ab[k].reshape(size, width), wp[...], preferred_element_type=F32)
        vx[me, chunk_slice(k), :] = (visual * flat(gain)).astype(BF)
        squares = jnp.broadcast_to(jnp.sum(visual * visual, axis=1, keepdims=True), (size, HD)).T
        ssq[k, 0] = squares[0:8]
        for d in range(1, groups):
            copy = remote(
                ssq.at[k, 0], ssq.at[k, d], sq_ss.at[k, d], sq_rs.at[k, d], {"mp": (me + d) % groups}
            )
            copy.start()
            sq.append(copy)
        gather = Gather(
            lambda s, k=k: vx.at[s, pl.ds(k * size, size)],
            vx.at[me, pl.ds(k * size, size)],
            gather_sems(1 + k),
            groups,
            me,
        )
        gather.start()
        vx_gathers.append(gather)

    tile = 256 if q_width % 256 == 0 else 128

    def slot_rows(slot):
        return pl.ds(pl.multiple_of(slot * model, 64), model)

    def add_cache(slot, span, first):
        term = jnp.dot(vx[slot, span, :], wc[slot_rows(slot), :], preferred_element_type=F32)
        kv_acc[span, :] = term if first else kv_acc[span, :] + term

    def add_query(slot, span, first):
        for c in range(q_width // tile):
            cols = slice(c * tile, (c + 1) * tile)
            term = jnp.dot(vx[slot, span, :], wq[slot_rows(slot), cols], preferred_element_type=F32)
            q_acc[span, cols] = term if first else q_acc[span, cols] + term

    def turn(x, cos, sin):
        return x * cos + pltpu.roll(x, HD // 2, 1) * sin

    def finish_cache(k):
        span = chunk_slice(k)
        square_sum = ssq[k, 0]
        for d in range(1, groups):
            sq[k * (groups - 1) + d - 1].wait_recv()
            square_sum = square_sum + ssq[k, d]
        scale_row = lax.rsqrt(square_sum * (1.0 / (model * groups)) + epsilon)
        scale[span, :] = jnp.broadcast_to(scale_row[0:1], (HD, size)).T
        bias = flat(cache_bias)
        for i in range(ch):
            is_key = me * ch + i < KVH
            cols = slice(i * HD, (i + 1) * HD)
            state = kv_acc[span, cols] * scale[span, :] + bias[:, cols]
            cos = jnp.where(is_key, cosine[span, :], 1.0)
            sin = jnp.where(is_key, sine[span, :], 0.0)
            state = turn(state, cos, sin).astype(BF)
            kv[t, me, span, cols] = state
            key_value[span, cols] = state

    def finish_query(k):
        span = chunk_slice(k)
        bias = flat(query_bias)
        for i in range(q_heads):
            cols = slice(i * HD, (i + 1) * HD)
            state = q_acc[span, cols] * scale[span, :] + bias[:, cols]
            qs[i, span, :] = turn(state, cosine[span, :], sine[span, :]).astype(BF)

    table = shared_heads(groups, q_heads, ch)

    def share_copy(d, k, entry):
        source, target, first, count = entry
        block = kv.at[
            lax.rem(t + spans - d, spans), source, pl.ds(k * size, size), pl.ds(first * HD, count * HD)
        ]
        return remote(block, block, d_ss.at[d, k, target], d_rs.at[d, k, source], {"mp": target})

    def share(d, k):
        for entry in table:

            @pl.when(me == entry[0])
            def _(entry=entry):
                share_copy(d, k, entry).start()

    def share_wait(d, k):
        for entry in table:

            @pl.when(me == entry[1])
            def _(entry=entry):
                share_copy(d, k, entry).wait_recv()

    def share_drain(d, k):
        for entry in table:

            @pl.when(me == entry[0])
            def _(entry=entry):
                share_copy(d, k, entry).wait_send()

    def pass_copy(d, k):
        block = kv.at[lax.rem(t + spans - d, spans), me, pl.ds(k * size, size)]
        return remote(block, block, z_ss.at[d, k], z_rs.at[d + 1, k], {"tm": (t + 1) % spans})

    def arrive_copy(d, k):
        block = kv.at[lax.rem(t + spans - d, spans), me, pl.ds(k * size, size)]
        return remote(block, block, z_ss.at[d, k], z_rs.at[d, k], {"tm": (t + spans - 1) % spans})

    def hand_on(d, k):
        @pl.when(t < spans - 1)
        def _():
            pass_copy(d, k).start()

        share(d, k)

    def service(d, k):
        arrive_copy(d, k).wait_recv()
        hand_on(d, k)

    loads[6].wait()
    loads[7].wait()
    everything = slice(0, rows)
    add_cache(me, everything, True)
    add_query(me, everything, True)
    arrivals = [gather.arrivals() for gather in vx_gathers]
    for k in range(chunks):
        slot = next(arrivals[k])
    add_cache(slot, everything, False)
    add_query(slot, everything, False)
    for k in range(chunks):
        span = chunk_slice(k)
        slots = []
        for slot in arrivals[k]:
            add_cache(slot, span, False)
            slots.append(slot)
        finish_cache(k)
        hand_on(0, k)
        for slot in slots:
            add_query(slot, span, False)
        finish_query(k)
        if k == 0 and chunks > 1:

            @pl.when(t > 0)
            def _():
                service(1, 0)

    def service_all(d):
        for k in range(chunks):
            if k == 0 and chunks > 1:

                @pl.when(d > 1)
                def _():
                    service(d, 0)
            else:
                service(d, k)

    def attend(d, diagonal):
        j = lax.rem(t + spans - d, spans)

        @pl.loop(0, q_heads, unroll=3 if q_heads % 3 == 0 else 1)
        def _(i):
            g = (me * q_heads + i) // GROUP
            k_cols = pl.ds(pl.multiple_of(lax.rem(g, ch) * HD, HD), HD)
            keys = kv[j, g // ch, :, k_cols]
            values = kv[j, (KVH + g) // ch, :, pl.ds(pl.multiple_of(lax.rem(KVH + g, ch) * HD, HD), HD)]
            scores = lax.dot_general(
                qs[i], keys, (((1,), (1,)), ((), ())), preferred_element_type=F32
            ) * (HD ** -0.5 * 1.4426950408889634)
            if diagonal:
                q_pos = lax.broadcasted_iota(jnp.int32, (rows, rows), 0)
                k_pos = lax.broadcasted_iota(jnp.int32, (rows, rows), 1)
                scores = jnp.where(k_pos <= q_pos, scores, masked)
            top = jnp.max(scores, axis=1, keepdims=True)
            if diagonal:
                new_peak = jnp.broadcast_to(top, (rows, HD))
            else:
                new_peak = jnp.maximum(peak[i], top)
            weights = jnp.exp2(scores - new_peak[:, 0:1])
            added = jnp.sum(weights, axis=1, keepdims=True)
            product = jnp.dot(weights.astype(BF), values, preferred_element_type=F32)
            if diagonal:
                denom[i] = jnp.broadcast_to(added, (rows, HD))
                numer[i] = product
            else:
                rescale = jnp.exp2(peak[i] - new_peak)
                denom[i] = denom[i] * rescale + added
                numer[i] = numer[i] * rescale + product
            peak[i] = new_peak

    def share_wait_all(d):
        for k in range(chunks):
            share_wait(d, k)

    last = t == spans - 1

    @pl.when(t < spans - 1)
    def _():
        @pl.loop(1, t + 1)
        def _(d):
            service_all(d)

    @pl.when(last)
    def _():
        service_all(1)

    share_wait_all(0)
    attend(0, True)

    @pl.loop(1, t + 1)
    def _(d):
        @pl.when(last & (d < t))
        def _():
            service_all(d + 1)

        share_wait_all(d)
        attend(d, False)

    for i in range(q_heads):
        attention[:, i * HD : (i + 1) * HD] = (numer[i] / denom[i]).astype(BF)


    @pl.when(t < spans - 1)
    def _():
        for copy in up:
            copy.wait_send()

        @pl.loop(0, t + 1)
        def _(d):
            for k in range(chunks):
                pass_copy(d, k).wait_send()

    @pl.when(t > 0)
    def _():
        for copy in down:
            copy.wait_send()

    @pl.loop(0, t + 1)
    def _(d):
        for k in range(chunks):
            share_drain(d, k)

    wo_gather.drain()
    for gather in vx_gathers:
        gather.drain()
    for copy in rs + ab_copies + sq:
        copy.wait_send()
    for copies in exchange:
        for copy in copies:
            copy.wait_send()


def rows_first(x):
    return x.reshape(-1, HD) if x.shape[0] % HD == 0 else x[None]


def local(
    features,
    queries,
    anchor_frame,
    anchor_patch,
    time_offset,
    space_offset,
    value_weight,
    point_weight,
    point_bias,
    output_weight,
    project_weight,
    norm_gain,
    query_weight,
    query_bias,
    cache_weight,
    cache_bias,
):
    groups = lax.axis_size("mp")
    spans = lax.axis_size("tm")
    frames_here, patches_here, width = features.shape
    cells = frames_here * patches_here
    rows = queries.shape[0]
    chunks = max(1, rows // chunk_rows)
    size = rows // chunks
    part = size // 2
    frequency = rope_base ** (-2.0 * np.arange(HD // 2, dtype=np.float64) / HD)
    sign = np.concatenate([-np.ones(HD // 2), np.ones(HD // 2)])

    def turns(positions):
        angles = positions[:, None] * np.concatenate([frequency, frequency])[None, :]
        return jnp.asarray(np.stack([np.cos(angles), np.sin(angles) * sign]).astype(np.float32))

    row_turn = turns(np.arange(rows, dtype=np.float64))
    span_turn = turns(np.arange(spans, dtype=np.float64) * rows)
    model = project_weight.shape[1]
    q_width = query_weight.shape[1]
    c_width = cache_weight.shape[1]
    q_heads = q_width // HD
    chips = groups // 2
    vmem = pl.BlockSpec(memory_space=pltpu.VMEM)
    hbm = pl.BlockSpec(memory_space=pltpu.HBM)
    dma = pltpu.SemaphoreType.DMA
    V = pltpu.VMEM
    return tuple(
        pl.pallas_call(
            functools.partial(kernel, groups, spans, frames_here, chunks),
            out_shape=(
                jax.ShapeDtypeStruct((rows, q_width), BF),
                jax.ShapeDtypeStruct((rows, c_width), BF),
            ),
            in_specs=[hbm] * 3 + [vmem] * 10 + [hbm] * 5,
            out_specs=(vmem, vmem),
            scratch_shapes=[
                V((cells, width), BF),
                V((rows, width), BF),
                V((2, rows, HD), F32),
                V((width, width), BF),
                V((groups, width // groups, width), BF),
                V((width, model), BF),
                V(query_weight.shape, BF),
                V(cache_weight.shape, BF),
                V((4 * patches_here, width), BF),
                V((cells, width), BF),
                V((2 * patches_here, width), BF),
                V((rows, HD), F32),
                V((AH, 4 * POINTS, rows), F32),
                V((rows, HD), F32),
                V((rows, HD), F32),
                V((max(2, frames_here) * patches_here, rows), F32),
                V((rows, width), F32),
                V((chunks, part, width), BF),
                V((chunks, part, width), BF),
                V((chips, chunks, part, width), BF),
                V((chunks, 2, part, width), BF),
                V((groups, rows, model), BF),
                V((chunks, groups, 8, size), F32),
                V((rows, HD), F32),
                V((rows, q_width), F32),
                V((rows, c_width), F32),
                V((q_heads, rows, HD), BF),
                V((spans, groups, rows, c_width), BF),
                V((q_heads, rows, HD), F32),
                V((q_heads, rows, HD), F32),
                V((q_heads, rows, HD), F32),
                dma((8,)),
                dma((2, 2)),
                dma((2, 2)),
                dma((chunks,)),
                dma((chunks,)),
                dma((chunks, chips)),
                dma((chunks, chips)),
                dma((chunks,)),
                dma((chunks,)),
                dma((chunks, groups)),
                dma((chunks, groups)),
                dma((spans, chunks)),
                dma((spans, chunks)),
                dma((spans, chunks, groups)),
                dma((spans, chunks, groups)),
                dma((1 + chunks, 4, chips)),
            ],
            compiler_params=pltpu.CompilerParams(
                collective_id=0, has_side_effects=True, vmem_limit_bytes=48 * 1024 * 1024
            ),
        )(
            features.reshape(cells, width),
            queries,
            row_turn,
            anchor_frame[None],
            anchor_patch[None],
            time_offset.transpose(1, 2, 0),
            space_offset.transpose(0, 2, 3, 1),
            point_weight.T,
            point_bias[None],
            span_turn,
            rows_first(norm_gain),
            rows_first(query_bias),
            rows_first(cache_bias),
            value_weight,
            output_weight,
            project_weight,
            query_weight,
            cache_weight,
        )
    )


def solution(mesh):
    return jax.shard_map(
        local,
        mesh=mesh,
        in_specs=(
            P(("dp", "tm"), "mp", None),
            P(("dp", "tm"), None),
            P(("dp", "tm")),
            P(("dp", "tm")),
            P(("dp", "tm"), None, None),
            P(None, ("dp", "tm"), None, None),
            P(),
            P(),
            P(),
            P("mp", None),
            P(None, "mp"),
            P("mp"),
            P(None, "mp"),
            P("mp"),
            P(None, "mp"),
            P("mp"),
        ),
        out_specs=(P(("dp", "tm"), "mp"), P(("dp", "tm"), "mp")),
        check_vma=False,
    )
```

time: 101 us -> 75.6 us (0.75)
  Pallas kernels: 87.6 us -> 60 us
  local copies, waits for them, and re-layouts: 6.64 us -> 14.4 us
  other arithmetic: 4.42 us -> 0 us
  matrix products: 1.31 us -> 0 us
    pallas_call x1, Pallas kernels: 87.6 us -> 60 us  [local(): pl.pallas_call(functools.partial(kernel, groups, spans, frames_here, chun...]
    unnamed x4 -> x32, local copies, waits for them, and re-layouts: 3.34 us -> 14.4 us
    broadcast_in_dim x2 -> x0, local copies, waits for them, and re-layouts: 2.55 us -> none  [the longest x1 1.28 us: local(): norm_gain[None]]
    convert_element_type x3 -> x0, other arithmetic: 1.38 us -> none  [the longest x1 0.69 us: local(): (anchor_patch // GRID).astype(F32)[:, None, None] + space_offset[0]]
    dot_general x1 -> x0, matrix products: 1.31 us -> none  [local(): jnp.dot(queries, point_weight, preferred_element_type=F32) + point_bias]
where the time goes in v1:
time: 75.6 us; the launch traced here: 75 us
  Pallas kernels  60 us (79%)
  local copies, waits for them, and re-layouts  14.4 us (19%)
    pallas_call x1, Pallas kernels, local(): pl.pallas_call(functools.partial(kernel, groups, spans, frames_here, chun...  60 us
    unnamed x32, local copies, waits for them, and re-layouts  14.4 us

profile of v1, /device:TPU:27, one launch (start us, length us, event | category | flops | bytes accessed | tf_op | source)
XLA Modules:
  0.0 75.0 jit_solution(12930593659282679990)
XLA Ops:
  0.6 0.0 copy-start
  0.6 1.5 %copy-done = bf16[1024,896]{1,0:T(8,128)(2,1)S(1)} copy-done((bf16[1024,896]{1,0:T(8,128)(2,1)S(1)}, bf16[1024,896]{1,0:T(8,128)(2,1)}, u32[]{:S(2)}) %copy-start) | copy-done | bytes 1835032
  2.1 0.0 copy-start.1
  2.1 1.3 %copy-done.1 = bf16[4,144,1024]{2,1,0:T(8,128)(2,1)S(1)} copy-done((bf16[4,144,1024]{2,1,0:T(8,128)(2,1)S(1)}, bf16[4,144,1024]{2,1,0:T(8,128)(2,1)}, u32[]{:S(2)}) %copy-start.1) | copy-done | bytes 1179672
  3.4 0.0 copy-start.2
  3.4 1.0 %copy-done.2 = bf16[256,1024]{1,0:T(8,128)(2,1)S(1)} copy-done((bf16[256,1024]{1,0:T(8,128)(2,1)S(1)}, bf16[256,1024]{1,0:T(8,128)(2,1)}, u32[]{:S(2)}) %copy-start.2) | copy-done | bytes 524312
  4.5 0.0 copy-start.3
  4.5 1.0 %copy-done.3 = bf16[256,1024]{1,0:T(8,128)(2,1)S(1)} copy-done((bf16[256,1024]{1,0:T(8,128)(2,1)S(1)}, bf16[256,1024]{1,0:T(8,128)(2,1)}, u32[]{:S(2)}) %copy-start.3) | copy-done | bytes 524312
  5.5 0.0 copy-start.4
  5.5 0.9 %copy-done.4 = f32[2,256,128]{2,1,0:T(8,128)S(1)} copy-done((f32[2,256,128]{2,1,0:T(8,128)S(1)}, f32[2,256,128]{2,1,0:T(8,128)}, u32[]{:S(2)}) %copy-start.4) | copy-done | bytes 262168
  6.4 0.0 copy-start.5
  6.4 0.8 %copy-done.5 = f32[2,256,8,4]{1,3,2,0:T(4,128)S(1)} copy-done((f32[2,256,8,4]{1,3,2,0:T(4,128)S(1)}, f32[2,256,8,4]{1,3,2,0:T(4,128)}, u32[]{:S(2)}) %copy-start.5) | copy-done | bytes 65560
  7.3 0.8 %copy-done.6 = bf16[1024,32]{0,1:T(8,128)(2,1)S(1)} copy-done((bf16[1024,32]{0,1:T(8,128)(2,1)S(1)}, bf16[1024,32]{0,1:T(8,128)(2,1)}, u32[]{:S(2)}) %copy-start.6) | copy-done | bytes 65560
  8.1 0.8 %copy-done.7 = f32[256,8,4]{0,2,1:T(4,128)S(1)} copy-done((f32[256,8,4]{0,2,1:T(4,128)S(1)}, f32[256,8,4]{0,2,1:T(4,128)}, u32[]{:S(2)}) %copy-start.7) | copy-done | bytes 32792
  8.9 0.7 copy-done.8
  9.6 0.7 copy-done.9
  10.3 0.7 copy-done.10
  10.9 0.7 copy-done.11
  11.6 0.7 copy-done.12
  12.3 0.7 copy-done.13
  13.0 0.7 copy-done.14
  13.6 60.0 %shard_map.185 = (bf16[256,768]{1,0:T(8,128)(2,1)S(1)}, bf16[256,256]{1,0:T(8,128)(2,1)S(1)}) custom-call(bf16[576,1024]{1,0:T(8,128)(2,1)S(1)} %bitcast.10, bf16[256,1024]{1,0:T(8,128)(2,1)S(1)} %copy-done.2, f32[2,256,128]{2,1,0:T(8,128)S(1)} %copy-done.4, s32[1,256]{1,0:T(1,128)S(1)} %bitcast.16, s32[1,256]{1,0:T(1,128)S(1)} %bitcast.17, ...), custom_call_target="tpu_custom_call" | custom-call | tf_op jit(solution)/shard_map/pallas_call | solution.py:686
  73.6 0.7 copy.22
  74.4 0.7 copy.23
  (9 shorter events, 0.0 us)
Async XLA Ops:
  0.6 1.5 %copy-start = (bf16[1024,896]{1,0:T(8,128)(2,1)S(1)}, bf16[1024,896]{1,0:T(8,128)(2,1)}, u32[]{:S(2)}) copy-start(bf16[1024,896]{1,0:T(8,128)(2,1)} %project_hbm.1) | copy-start | bytes 5505028
  2.1 1.3 %copy-start.1 = (bf16[4,144,1024]{2,1,0:T(8,128)(2,1)S(1)}, bf16[4,144,1024]{2,1,0:T(8,128)(2,1)}, u32[]{:S(2)}) copy-start(bf16[4,144,1024]{2,1,0:T(8,128)(2,1)} %param.18) | copy-start | bytes 3538948
  3.4 1.0 %copy-start.2 = (bf16[256,1024]{1,0:T(8,128)(2,1)S(1)}, bf16[256,1024]{1,0:T(8,128)(2,1)}, u32[]{:S(2)}) copy-start(bf16[256,1024]{1,0:T(8,128)(2,1)} %queries_hbm.1) | copy-start | bytes 1572868
  4.5 1.0 %copy-start.3 = (bf16[256,1024]{1,0:T(8,128)(2,1)S(1)}, bf16[256,1024]{1,0:T(8,128)(2,1)}, u32[]{:S(2)}) copy-start(bf16[256,1024]{1,0:T(8,128)(2,1)} %output_hbm.1) | copy-start | bytes 1572868
  5.5 0.9 %copy-start.4 = (f32[2,256,128]{2,1,0:T(8,128)S(1)}, f32[2,256,128]{2,1,0:T(8,128)}, u32[]{:S(2)}) copy-start(f32[2,256,128]{2,1,0:T(8,128)} %constant.4.clone.row_turn_hbm) | copy-start | bytes 786436
  6.4 0.8 %copy-start.5 = (f32[2,256,8,4]{1,3,2,0:T(4,128)S(1)}, f32[2,256,8,4]{1,3,2,0:T(4,128)}, u32[]{:S(2)}) copy-start(f32[2,256,8,4]{1,3,2,0:T(4,128)} %param.23) | copy-start | bytes 196612
  7.3 0.8 %copy-start.6 = (bf16[1024,32]{0,1:T(8,128)(2,1)S(1)}, bf16[1024,32]{0,1:T(8,128)(2,1)}, u32[]{:S(2)}) copy-start(bf16[1024,32]{0,1:T(8,128)(2,1)} %param.25) | copy-start | bytes 196612
  8.1 0.8 %copy-start.7 = (f32[256,8,4]{0,2,1:T(4,128)S(1)}, f32[256,8,4]{0,2,1:T(4,128)}, u32[]{:S(2)}) copy-start(f32[256,8,4]{0,2,1:T(4,128)} %param.22) | copy-start | bytes 98308
  8.9 0.7 copy-start.8
  9.6 0.7 copy-start.9
  10.3 0.7 copy-start.10
  10.9 0.7 copy-start.11
  11.6 0.7 copy-start.12
  12.3 0.7 copy-start.13
  13.0 0.7 copy-start.14

commit v2 on v1

--- a/solution.py
+++ b/solution.py
@@ -744,24 +744,29 @@
                 collective_id=0, has_side_effects=True, vmem_limit_bytes=48 * 1024 * 1024
             ),
         )(
-            features.reshape(cells, width),
-            queries,
-            row_turn,
-            anchor_frame[None],
-            anchor_patch[None],
-            time_offset.transpose(1, 2, 0),
-            space_offset.transpose(0, 2, 3, 1),
-            point_weight.T,
-            point_bias[None],
-            span_turn,
-            rows_first(norm_gain),
-            rows_first(query_bias),
-            rows_first(cache_bias),
-            value_weight,
-            output_weight,
-            project_weight,
-            query_weight,
-            cache_weight,
+            *[
+                pltpu.with_memory_space_constraint(x, pltpu.HBM)
+                for x in (
+                    features.reshape(cells, width),
+                    queries,
+                    row_turn,
+                    anchor_frame[None],
+                    anchor_patch[None],
+                    time_offset.transpose(1, 2, 0),
+                    space_offset.transpose(0, 2, 3, 1),
+                    point_weight.T,
+                    point_bias[None],
+                    span_turn,
+                    rows_first(norm_gain),
+                    rows_first(query_bias),
+                    rows_first(cache_bias),
+                    value_weight,
+                    output_weight,
+                    project_weight,
+                    query_weight,
+                    cache_weight,
+                )
+            ]
         )
     )
 

time: 75.6 us -> 62.9 us (0.83)
  local copies, waits for them, and re-layouts: 14.4 us -> 1.4 us
    unnamed x32 -> x2, local copies, waits for them, and re-layouts: 14.4 us -> 1.4 us
where the time goes in v2:
time: 62.9 us; the launch traced here: 62.7 us
  Pallas kernels  60.6 us (96%)
  local copies, waits for them, and re-layouts  1.4 us (2%)
  between operations  0.65 us (1%)
    pallas_call x1, Pallas kernels, local(): pl.pallas_call(functools.partial(kernel, groups, spans, frames_here, chun...  60.6 us
    unnamed x2, local copies, waits for them, and re-layouts  1.4 us

profile of v2, /device:TPU:27, one launch (start us, length us, event | category | flops | bytes accessed | tf_op | source)
XLA Modules:
  0.0 62.7 jit_solution(9514961072191314124)
XLA Ops:
  0.6 60.6 %shard_map.185 = (bf16[256,768]{1,0:T(8,128)(2,1)S(1)}, bf16[256,256]{1,0:T(8,128)(2,1)S(1)}) custom-call(bf16[576,1024]{1,0:T(8,128)(2,1)} %bitcast.10, bf16[256,1024]{1,0:T(8,128)(2,1)} %queries_hbm.1, f32[2,256,128]{2,1,0:T(8,128)} %constant.4.clone.row_turn_hbm, s32[1,256]{1,0:T(1,128)} %bitcast.16, s32[1,256]{1,0:T(1,128)} %bitcast.17, ...), custom_call_target="tpu_custom_call" | custom-call | tf_op jit(solution)/shard_map/pallas_call | solution.py:686
  61.3 0.7 %copy.22 = bf16[256,768]{1,0:T(8,128)(2,1)} copy(bf16[256,768]{1,0:T(8,128)(2,1)S(1)} %get-tuple-element.4) | data formatting | bytes 786432
  62.0 0.7 %copy.23 = bf16[256,256]{1,0:T(8,128)(2,1)} copy(bf16[256,256]{1,0:T(8,128)(2,1)S(1)} %get-tuple-element.5) | data formatting | bytes 262144

commit v3 on v2

--- a/solution.py
+++ b/solution.py
@@ -18,7 +18,7 @@
 rope_base = 1000000.0
 epsilon = 1e-06
 masked = -1e30
-chunk_rows = 128
+chunk_rows = 64
 MESH = pl.DeviceIdType.MESH
 BF = jnp.bfloat16
 F32 = jnp.float32
@@ -129,7 +129,8 @@
     coords,
     cosine,
     sine,
-    corner,
+    vw_turned,
+    sums,
     partial,
     rs_send,
     rs_recv,
@@ -177,6 +178,19 @@
     partner = me + 1 - 2 * core
     size = rows // chunks
     part = size // 2
+    padded = ssq.shape[3]
+
+    barrier = pltpu.get_barrier_semaphore()
+    for d in range(1, groups):
+        pl.semaphore_signal(barrier, inc=1, device_id={"mp": (me + d) % groups}, device_id_type=MESH)
+
+    @pl.when(t < spans - 1)
+    def _():
+        pl.semaphore_signal(barrier, inc=1, device_id={"tm": (t + 1) % spans}, device_id_type=MESH)
+
+    @pl.when(t > 0)
+    def _():
+        pl.semaphore_signal(barrier, inc=1, device_id={"tm": (t + spans - 1) % spans}, device_id_type=MESH)
 
     loads = [
         pltpu.make_async_copy(src, dst, load_sem.at[i])
@@ -195,18 +209,6 @@
     ]
     for load in loads:
         load.start()
-
-    barrier = pltpu.get_barrier_semaphore()
-    for d in range(1, groups):
-        pl.semaphore_signal(barrier, inc=1, device_id={"mp": (me + d) % groups}, device_id_type=MESH)
-
-    @pl.when(t < spans - 1)
-    def _():
-        pl.semaphore_signal(barrier, inc=1, device_id={"tm": (t + 1) % spans}, device_id_type=MESH)
-
-    @pl.when(t > 0)
-    def _():
-        pl.semaphore_signal(barrier, inc=1, device_id={"tm": (t + spans - 1) % spans}, device_id_type=MESH)
 
     neighbours = jnp.where(t > 0, 1, 0) + jnp.where(t < spans - 1, 1, 0)
     pl.semaphore_wait(barrier, groups - 1 + neighbours)
@@ -284,8 +286,10 @@
 
     def project_values(source, target):
         for c in range(width // 256):
-            cols = slice(c * 256, (c + 1) * 256)
-            target[:, cols] = jnp.dot(source[...], vw[:, cols], preferred_element_type=F32).astype(BF)
+            columns = slice(c * 256, (c + 1) * 256)
+            target[columns, :] = lax.dot_general(
+                vw_turned[columns, :], source[...], (((1,), (1,)), ((), ())), preferred_element_type=F32
+            ).astype(BF)
 
     line_index = lax.broadcasted_iota(jnp.int32, (GRID, rows), 0).astype(F32)
     first_line = (me * lines).astype(F32)
@@ -297,29 +301,28 @@
     def sample(values, offsets, head):
         info = coords[head]
         columns = [hat(info[8 + k : 9 + k], line_index) for k in range(POINTS)]
-        for f, offset in enumerate(offsets):
+        blocks = []
+        for offset in offsets:
             timed = info[12:16] * hat(info[0:4], first_frame + offset)
             for line in range(lines):
                 share = timed * hat(info[4:8], first_line + line)
                 total = share[0:1] * columns[0]
                 for k in range(1, POINTS):
                     total = total + share[k : k + 1] * columns[k]
-                corner[pl.ds((f * lines + line) * GRID, GRID), :] = total
-        cols = pl.ds(pl.multiple_of(head * HD, HD), HD)
-        return lax.dot_general(
-            corner[pl.ds(0, values.shape[0]), :].astype(BF),
-            values[:, cols],
-            (((0,), (0,)), ((), ())),
-            preferred_element_type=F32,
-        )
-
+                blocks.append(total)
+        corner = jnp.concatenate(blocks, axis=0).astype(BF)
+        mine = values[pl.ds(pl.multiple_of(head * HD, HD), HD), :]
+        return jnp.dot(mine, corner, preferred_element_type=F32)
+
+    for c in range(width // 256):
+        columns = slice(c * 256, (c + 1) * 256)
+        vw_turned[columns, :] = vw[:, columns].T
     project_values(own_features, own_values)
 
 
-    @pl.loop(0, AH)
+    @pl.loop(0, AH, unroll=2)
     def _(head):
-        cols = pl.ds(pl.multiple_of(head * HD, HD), HD)
-        partial[:, cols] = sample(own_values, range(frames), head)
+        sums[pl.ds(pl.multiple_of(head * HD, HD), HD), :] = sample(own_values, range(frames), head)
 
     loads[4].wait()
     span_cos, span_sin = span_turn[0, pl.ds(t, 1), :], span_turn[1, pl.ds(t, 1), :]
@@ -337,31 +340,38 @@
             down[i].wait_recv()
 
         both = pl.ds(2 * i * per_frame, 2 * per_frame)
+        if i == 1:
+            loads[3].wait()
+            wo_arrivals = wo_gather.arrivals()
+            for _ in range(2 * chips - 2):
+                next(wo_arrivals)
         project_values(halo.at[both], halo_values)
 
-        @pl.loop(0, AH)
+        @pl.loop(0, AH, unroll=2)
         def _(head, i=i):
-            cols = pl.ds(pl.multiple_of(head * HD, HD), HD)
-            partial[:, cols] = partial[:, cols] + sample(halo_values, (-1 - i, frames + i), head)
-
-        if i == 0:
-            loads[3].wait()
-            for _ in wo_gather.arrivals():
-                pass
-
-
-    def rows_of(k, which):
+            mine = pl.ds(pl.multiple_of(head * HD, HD), HD)
+            total = sums[mine, :] + sample(halo_values, (-1 - i, frames + i), head)
+            if i == 0:
+                sums[mine, :] = total
+            else:
+                partial[:, mine] = total.T
+
+
+    def part_rows(k, which):
         return pl.ds(pl.multiple_of(k * size + which * part, part), part)
+
+    def chunk_rows_of(k):
+        return pl.ds(k * size, size)
 
     rs = []
     for k in range(chunks):
-        rs_send[k] = partial[rows_of(k, 1 - core), :].astype(BF)
+        rs_send[k] = partial[part_rows(k, 1 - core), :].astype(BF)
         rs.append(remote(rs_send.at[k], rs_recv.at[k], rs_ss.at[k], rs_rs.at[k], {"mp": partner}))
         rs[k].start()
     exchange = []
     for k in range(chunks):
         rs[k].wait_recv()
-        ex[chip, k] = (partial[rows_of(k, core), :] + rs_recv[k].astype(F32)).astype(BF)
+        ex[chip, k] = (partial[part_rows(k, core), :] + rs_recv[k].astype(F32)).astype(BF)
         copies = []
         for d in range(1, chips):
             mine = ex.at[chip, k]
@@ -371,33 +381,30 @@
             copies[-1].start()
         exchange.append(copies)
     loads[5].wait()
+    for _ in wo_arrivals:
+        pass
 
     def chunk_slice(k):
         return slice(k * size, (k + 1) * size)
 
     vx_gathers, ab_copies, sq = [], [], []
-    for k in range(chunks):
+
+    def mix(k):
         for copy in exchange[k]:
             copy.wait_recv()
         total = ex[0, k].astype(F32)
         for c in range(1, chips):
             total = total + ex[c, k].astype(F32)
         mixed = jnp.dot(total.astype(BF), wo[...].reshape(width, width), preferred_element_type=F32)
-        ab[k, core] = (queries[rows_of(k, core), :].astype(F32) + mixed).astype(BF)
+        ab[k, core] = (queries[part_rows(k, core), :].astype(F32) + mixed).astype(BF)
         mine = ab.at[k, core]
         ab_copies.append(remote(mine, mine, ab_ss.at[k], ab_rs.at[k], {"mp": partner}))
         ab_copies[k].start()
+
+    def project(k):
         ab_copies[k].wait_recv()
         visual = jnp.dot(ab[k].reshape(size, width), wp[...], preferred_element_type=F32)
         vx[me, chunk_slice(k), :] = (visual * flat(gain)).astype(BF)
-        squares = jnp.broadcast_to(jnp.sum(visual * visual, axis=1, keepdims=True), (size, HD)).T
-        ssq[k, 0] = squares[0:8]
-        for d in range(1, groups):
-            copy = remote(
-                ssq.at[k, 0], ssq.at[k, d], sq_ss.at[k, d], sq_rs.at[k, d], {"mp": (me + d) % groups}
-            )
-            copy.start()
-            sq.append(copy)
         gather = Gather(
             lambda s, k=k: vx.at[s, pl.ds(k * size, size)],
             vx.at[me, pl.ds(k * size, size)],
@@ -405,8 +412,22 @@
             groups,
             me,
         )
+        squares = jnp.broadcast_to(jnp.sum(visual * visual, axis=1, keepdims=True), (size, HD))
+        if padded > size:
+            squares = jnp.concatenate([squares, jnp.zeros((padded - size, HD), F32)], axis=0)
+        ssq[k, 0] = squares.T[0:8]
+        for d in range(1, groups):
+            copy = remote(
+                ssq.at[k, 0], ssq.at[k, d], sq_ss.at[k, d], sq_rs.at[k, d], {"mp": (me + d) % groups}
+            )
+            copy.start()
+            sq.append(copy)
         gather.start()
         vx_gathers.append(gather)
+
+    for k in range(chunks):
+        mix(k)
+        project(k)
 
     tile = 256 if q_width % 256 == 0 else 128
 
@@ -433,7 +454,7 @@
             sq[k * (groups - 1) + d - 1].wait_recv()
             square_sum = square_sum + ssq[k, d]
         scale_row = lax.rsqrt(square_sum * (1.0 / (model * groups)) + epsilon)
-        scale[span, :] = jnp.broadcast_to(scale_row[0:1], (HD, size)).T
+        scale[span, :] = jnp.broadcast_to(scale_row[0:1], (HD, padded)).T[0:size]
         bias = flat(cache_bias)
         for i in range(ch):
             is_key = me * ch + i < KVH
@@ -523,20 +544,18 @@
         for slot in slots:
             add_query(slot, span, False)
         finish_query(k)
-        if k == 0 and chunks > 1:
-
-            @pl.when(t > 0)
-            def _():
-                service(1, 0)
-
-    def service_all(d):
+        for d in range(1, min(k, spans - 1) + 1):
+
+            @pl.when(t >= d)
+            def _(d=d, k=k):
+                service(d, k - d)
+
+    def wave(w):
         for k in range(chunks):
-            if k == 0 and chunks > 1:
-
-                @pl.when(d > 1)
-                def _():
-                    service(d, 0)
-            else:
+            d = w - k
+
+            @pl.when((d >= 1) & (d <= t))
+            def _(d=d, k=k):
                 service(d, k)
 
     def attend(d, diagonal):
@@ -580,13 +599,13 @@
 
     @pl.when(t < spans - 1)
     def _():
-        @pl.loop(1, t + 1)
-        def _(d):
-            service_all(d)
-
-    @pl.when(last)
-    def _():
-        service_all(1)
+        @pl.loop(chunks, chunks + t)
+        def _(w):
+            wave(w)
+
+    @pl.when(last & (t > 0))
+    def _():
+        wave(chunks)
 
     share_wait_all(0)
     attend(0, True)
@@ -595,7 +614,7 @@
     def _(d):
         @pl.when(last & (d < t))
         def _():
-            service_all(d + 1)
+            wave(chunks + d)
 
         share_wait_all(d)
         attend(d, False)
@@ -701,20 +720,21 @@
                 V(query_weight.shape, BF),
                 V(cache_weight.shape, BF),
                 V((4 * patches_here, width), BF),
-                V((cells, width), BF),
-                V((2 * patches_here, width), BF),
+                V((width, cells), BF),
+                V((width, 2 * patches_here), BF),
                 V((rows, HD), F32),
                 V((AH, 4 * POINTS, rows), F32),
                 V((rows, HD), F32),
                 V((rows, HD), F32),
-                V((max(2, frames_here) * patches_here, rows), F32),
+                V((width, width), BF),
+                V((width, rows), F32),
                 V((rows, width), F32),
                 V((chunks, part, width), BF),
                 V((chunks, part, width), BF),
                 V((chips, chunks, part, width), BF),
                 V((chunks, 2, part, width), BF),
                 V((groups, rows, model), BF),
-                V((chunks, groups, 8, size), F32),
+                V((chunks, groups, 8, -(-size // HD) * HD), F32),
                 V((rows, HD), F32),
                 V((rows, q_width), F32),
                 V((rows, c_width), F32),

time: 62.9 us -> 64.5 us (1.025)
  Pallas kernels: 60.6 us -> 62.3 us
    pallas_call x1, Pallas kernels: 60.6 us -> 62.3 us  [local(): pl.pallas_call(functools.partial(kernel, groups, spans, frames_here, chun...]
where the time goes in v3:
time: 64.5 us; the launch traced here: 64.3 us
  Pallas kernels  62.3 us (97%)
  local copies, waits for them, and re-layouts  1.4 us (2%)
  between operations  0.65 us (1%)
    pallas_call x1, Pallas kernels, local(): pl.pallas_call(functools.partial(kernel, groups, spans, frames_here, chun...  62.3 us
    unnamed x2, local copies, waits for them, and re-layouts  1.4 us

profile of v3, /device:TPU:27, one launch (start us, length us, event | category | flops | bytes accessed | tf_op | source)
XLA Modules:
  0.0 64.3 jit_solution(4751357629588937603)
XLA Ops:
  0.6 62.3 %shard_map.185 = (bf16[256,768]{1,0:T(8,128)(2,1)S(1)}, bf16[256,256]{1,0:T(8,128)(2,1)S(1)}) custom-call(bf16[576,1024]{1,0:T(8,128)(2,1)} %bitcast.10, bf16[256,1024]{1,0:T(8,128)(2,1)} %queries_hbm.1, f32[2,256,128]{2,1,0:T(8,128)} %constant.4.clone.row_turn_hbm, s32[1,256]{1,0:T(1,128)} %bitcast.16, s32[1,256]{1,0:T(1,128)} %bitcast.17, ...), custom_call_target="tpu_custom_call" | custom-call | tf_op jit(solution)/shard_map/pallas_call | solution.py:705
  62.9 0.7 %copy.22 = bf16[256,768]{1,0:T(8,128)(2,1)} copy(bf16[256,768]{1,0:T(8,128)(2,1)S(1)} %get-tuple-element.4) | data formatting | bytes 786432
  63.7 0.7 %copy.23 = bf16[256,256]{1,0:T(8,128)(2,1)} copy(bf16[256,256]{1,0:T(8,128)(2,1)S(1)} %get-tuple-element.5) | data formatting | bytes 262144

commit v4 on v3

--- a/solution.py
+++ b/solution.py
@@ -18,7 +18,6 @@
 rope_base = 1000000.0
 epsilon = 1e-06
 masked = -1e30
-chunk_rows = 64
 MESH = pl.DeviceIdType.MESH
 BF = jnp.bfloat16
 F32 = jnp.float32
@@ -74,6 +73,10 @@
             copy.wait_send()
 
 
+def row_chunks(rows):
+    return ((0, 3 * rows // 8), (3 * rows // 8, 3 * rows // 8), (3 * rows // 4, rows // 4))
+
+
 def shared_heads(groups, q_heads, ch):
     table = []
     for source in range(groups):
@@ -81,7 +84,9 @@
             wanted = {(target * q_heads + i) // GROUP for i in range(q_heads)}
             need = [h for h in range(ch) if (source * ch + h) % KVH in wanted]
             if target != source and need:
-                table.append((source, target, need[0], need[-1] - need[0] + 1))
+                sent = sum(e[0] == source for e in table)
+                received = sum(e[1] == target for e in table)
+                table.append((source, target, need[0], need[-1] - need[0] + 1, sent, received))
     return table
 
 
@@ -93,7 +98,7 @@
     groups,
     spans,
     frames,
-    chunks,
+    plan,
     features,
     queries_hbm,
     row_turn_hbm,
@@ -112,6 +117,8 @@
     project_hbm,
     query_hbm,
     cache_hbm,
+    attention_out,
+    key_value_out,
     attention,
     key_value,
     own_features,
@@ -147,6 +154,7 @@
     denom,
     numer,
     load_sem,
+    out_sem,
     halo_ss,
     halo_rs,
     rs_ss,
@@ -176,21 +184,15 @@
     chips = groups // 2
     chip, core = me // 2, me % 2
     partner = me + 1 - 2 * core
-    size = rows // chunks
-    part = size // 2
+    chunks = len(plan)
     padded = ssq.shape[3]
 
     barrier = pltpu.get_barrier_semaphore()
     for d in range(1, groups):
         pl.semaphore_signal(barrier, inc=1, device_id={"mp": (me + d) % groups}, device_id_type=MESH)
 
-    @pl.when(t < spans - 1)
-    def _():
-        pl.semaphore_signal(barrier, inc=1, device_id={"tm": (t + 1) % spans}, device_id_type=MESH)
-
-    @pl.when(t > 0)
-    def _():
-        pl.semaphore_signal(barrier, inc=1, device_id={"tm": (t + spans - 1) % spans}, device_id_type=MESH)
+    for d in range(1, spans):
+        pl.semaphore_signal(barrier, inc=1, device_id={"tm": (t + d) % spans}, device_id_type=MESH)
 
     loads = [
         pltpu.make_async_copy(src, dst, load_sem.at[i])
@@ -210,8 +212,7 @@
     for load in loads:
         load.start()
 
-    neighbours = jnp.where(t > 0, 1, 0) + jnp.where(t < spans - 1, 1, 0)
-    pl.semaphore_wait(barrier, groups - 1 + neighbours)
+    pl.semaphore_wait(barrier, groups + spans - 2)
 
     up, down = [], []
     for i in range(2):
@@ -245,7 +246,8 @@
             copy.start()
 
     def gather_sems(index):
-        return [functools.partial(lambda k, d: ag_sem.at[index, k, d], k) for k in range(4)]
+        firsts = (-1, chips - 2, 2 * chips - 2, 3 * chips - 2)
+        return [functools.partial(lambda first, d: ag_sem.at[index, first + d], first) for first in firsts]
 
     wo_gather = Gather(lambda s: wo.at[s], output_hbm, gather_sems(0), groups, me)
     wo_gather.start()
@@ -329,6 +331,11 @@
     cosine[...] = span_cos * row_turn[0] - span_sin * row_turn[1]
     sine[...] = span_sin * row_turn[0] + span_cos * row_turn[1]
 
+    for i in range(q_heads):
+        peak[i] = jnp.full((1, rows), masked, F32)
+        denom[i] = jnp.zeros((1, rows), F32)
+        numer[i] = jnp.zeros((HD, rows), F32)
+
     for i in range(2):
 
         @pl.when(t > 0)
@@ -358,76 +365,99 @@
 
 
     def part_rows(k, which):
-        return pl.ds(pl.multiple_of(k * size + which * part, part), part)
-
-    def chunk_rows_of(k):
-        return pl.ds(k * size, size)
+        start, size = plan[k]
+        return pl.ds(pl.multiple_of(start + which * (size // 2), 16), size // 2)
+
+    def half_rows(k):
+        start, size = plan[k]
+        return pl.ds(start // 2, size // 2)
+
+    def chunk_slice(k):
+        start, size = plan[k]
+        return slice(start, start + size)
+
+    def chunk_span(k):
+        return pl.ds(*plan[k])
 
     rs = []
     for k in range(chunks):
-        rs_send[k] = partial[part_rows(k, 1 - core), :].astype(BF)
-        rs.append(remote(rs_send.at[k], rs_recv.at[k], rs_ss.at[k], rs_rs.at[k], {"mp": partner}))
+        rs_send[half_rows(k), :] = partial[part_rows(k, 1 - core), :].astype(BF)
+        rs.append(
+            remote(
+                rs_send.at[half_rows(k)], rs_recv.at[half_rows(k)], rs_ss.at[k], rs_rs.at[k], {"mp": partner}
+            )
+        )
         rs[k].start()
     exchange = []
-    for k in range(chunks):
+
+    def send_sums(k):
         rs[k].wait_recv()
-        ex[chip, k] = (partial[part_rows(k, core), :] + rs_recv[k].astype(F32)).astype(BF)
+        ex[chip, half_rows(k), :] = (
+            partial[part_rows(k, core), :] + rs_recv[half_rows(k), :].astype(F32)
+        ).astype(BF)
+        if k > 0:
+            for copy in exchange[k - 1]:
+                copy.wait_send()
         copies = []
         for d in range(1, chips):
-            mine = ex.at[chip, k]
+            mine = ex.at[chip, half_rows(k)]
             copies.append(
-                remote(mine, mine, ex_ss.at[k, d], ex_rs.at[k, d], {"mp": (chip + d) % chips * 2 + core})
+                remote(mine, mine, ex_ss.at[k, d - 1], ex_rs.at[k, d - 1], {"mp": (chip + d) % chips * 2 + core})
             )
             copies[-1].start()
         exchange.append(copies)
+
+    send_sums(0)
+    if chunks > 1:
+        send_sums(1)
     loads[5].wait()
     for _ in wo_arrivals:
         pass
 
-    def chunk_slice(k):
-        return slice(k * size, (k + 1) * size)
-
     vx_gathers, ab_copies, sq = [], [], []
 
     def mix(k):
         for copy in exchange[k]:
             copy.wait_recv()
-        total = ex[0, k].astype(F32)
+        total = ex[0, half_rows(k), :].astype(F32)
         for c in range(1, chips):
-            total = total + ex[c, k].astype(F32)
+            total = total + ex[c, half_rows(k), :].astype(F32)
         mixed = jnp.dot(total.astype(BF), wo[...].reshape(width, width), preferred_element_type=F32)
-        ab[k, core] = (queries[part_rows(k, core), :].astype(F32) + mixed).astype(BF)
-        mine = ab.at[k, core]
+        ab[part_rows(k, core), :] = (queries[part_rows(k, core), :].astype(F32) + mixed).astype(BF)
+        mine = ab.at[part_rows(k, core)]
         ab_copies.append(remote(mine, mine, ab_ss.at[k], ab_rs.at[k], {"mp": partner}))
         ab_copies[k].start()
 
     def project(k):
         ab_copies[k].wait_recv()
-        visual = jnp.dot(ab[k].reshape(size, width), wp[...], preferred_element_type=F32)
+        size = plan[k][1]
+        visual = jnp.dot(ab[chunk_slice(k), :], wp[...], preferred_element_type=F32)
         vx[me, chunk_slice(k), :] = (visual * flat(gain)).astype(BF)
         gather = Gather(
-            lambda s, k=k: vx.at[s, pl.ds(k * size, size)],
-            vx.at[me, pl.ds(k * size, size)],
+            lambda s, k=k: vx.at[s, chunk_span(k)],
+            vx.at[me, chunk_span(k)],
             gather_sems(1 + k),
             groups,
             me,
         )
         squares = jnp.broadcast_to(jnp.sum(visual * visual, axis=1, keepdims=True), (size, HD))
-        if padded > size:
-            squares = jnp.concatenate([squares, jnp.zeros((padded - size, HD), F32)], axis=0)
-        ssq[k, 0] = squares.T[0:8]
+        extra = -size % HD
+        if extra:
+            squares = jnp.concatenate([squares, jnp.zeros((extra, HD), F32)], axis=0)
+        ssq[k, 0, :, 0 : size + extra] = squares.T[0:8]
         for d in range(1, groups):
-            copy = remote(
-                ssq.at[k, 0], ssq.at[k, d], sq_ss.at[k, d], sq_rs.at[k, d], {"mp": (me + d) % groups}
-            )
+            remote(ssq.at[k, 0], ssq.at[k, d], sq_ss.at[k], sq_rs.at[k], {"mp": (me + d) % groups}).start()
+        rest = ssq.at[k, pl.ds(1, groups - 1)]
+        sq.append(remote(rest, rest, sq_ss.at[k], sq_rs.at[k], {"mp": partner}))
+        gather.near[0].start()
+        vx_gathers.append(gather)
+
+    def send_cross(k):
+        if k > 0:
+            for copy in vx_gathers[k - 1].cross[1:]:
+                copy.wait_send()
+        for copy in vx_gathers[k].cross[1:]:
             copy.start()
-            sq.append(copy)
-        gather.start()
-        vx_gathers.append(gather)
-
-    for k in range(chunks):
-        mix(k)
-        project(k)
 
     tile = 256 if q_width % 256 == 0 else 128
 
@@ -450,11 +480,11 @@
     def finish_cache(k):
         span = chunk_slice(k)
         square_sum = ssq[k, 0]
+        sq[k].wait_recv()
         for d in range(1, groups):
-            sq[k * (groups - 1) + d - 1].wait_recv()
             square_sum = square_sum + ssq[k, d]
         scale_row = lax.rsqrt(square_sum * (1.0 / (model * groups)) + epsilon)
-        scale[span, :] = jnp.broadcast_to(scale_row[0:1], (HD, padded)).T[0:size]
+        scale[span, :] = jnp.broadcast_to(scale_row[0:1], (HD, padded)).T[0 : plan[k][1]]
         bias = flat(cache_bias)
         for i in range(ch):
             is_key = me * ch + i < KVH
@@ -472,83 +502,163 @@
         for i in range(q_heads):
             cols = slice(i * HD, (i + 1) * HD)
             state = q_acc[span, cols] * scale[span, :] + bias[:, cols]
-            qs[i, span, :] = turn(state, cosine[span, :], sine[span, :]).astype(BF)
+            state = turn(state, cosine[span, :], sine[span, :]) * (HD ** -0.5 * 1.4426950408889634)
+            qs[i, span, :] = state.astype(BF)
 
     table = shared_heads(groups, q_heads, ch)
 
-    def share_copy(d, k, entry):
-        source, target, first, count = entry
-        block = kv.at[
-            lax.rem(t + spans - d, spans), source, pl.ds(k * size, size), pl.ds(first * HD, count * HD)
-        ]
-        return remote(block, block, d_ss.at[d, k, target], d_rs.at[d, k, source], {"mp": target})
+    early = pl.ds(0, plan[-1][0])
+
+    def share_copy(d, which, span, entry):
+        source, target, first, count, sent, received = entry
+        block = kv.at[lax.rem(t + spans - d, spans), source, span, pl.ds(first * HD, count * HD)]
+        return remote(block, block, d_ss.at[d, sent], d_rs.at[d, which, received], {"mp": target})
 
     def share(d, k):
         for entry in table:
 
             @pl.when(me == entry[0])
             def _(entry=entry):
-                share_copy(d, k, entry).start()
-
-    def share_wait(d, k):
+                share_copy(d, k // (chunks - 1), chunk_span(k), entry).start()
+
+    def share_wait(d, which):
         for entry in table:
 
             @pl.when(me == entry[1])
             def _(entry=entry):
-                share_copy(d, k, entry).wait_recv()
-
-    def share_drain(d, k):
+                share_copy(d, which, chunk_span(chunks - 1) if which else early, entry).wait_recv()
+
+    def share_drain(d):
         for entry in table:
 
             @pl.when(me == entry[0])
             def _(entry=entry):
-                share_copy(d, k, entry).wait_send()
+                share_copy(d, 0, pl.ds(0, rows), entry).wait_send()
+
+    def block_of(d, k):
+        return kv.at[lax.rem(t + spans - d, spans), me, chunk_span(k)]
 
     def pass_copy(d, k):
-        block = kv.at[lax.rem(t + spans - d, spans), me, pl.ds(k * size, size)]
-        return remote(block, block, z_ss.at[d, k], z_rs.at[d + 1, k], {"tm": (t + 1) % spans})
-
-    def arrive_copy(d, k):
-        block = kv.at[lax.rem(t + spans - d, spans), me, pl.ds(k * size, size)]
-        return remote(block, block, z_ss.at[d, k], z_rs.at[d, k], {"tm": (t + spans - 1) % spans})
-
-    def hand_on(d, k):
+        block = block_of(d, k)
+        return remote(block, block, z_ss.at[d + 1], z_rs.at[d + 1, k], {"tm": (t + 1) % spans})
+
+    def pass_on(d, k):
         @pl.when(t < spans - 1)
         def _():
             pass_copy(d, k).start()
 
+    def hand_on(k):
+        pass_on(0, k)
+        share(0, k)
+
+    def service(d, k):
+        block = block_of(d, k)
+        remote(block, block, z_ss.at[d], z_rs.at[d, k], {"tm": (t + spans - 1) % spans}).wait_recv()
+        pass_on(d, k)
         share(d, k)
 
-    def service(d, k):
-        arrive_copy(d, k).wait_recv()
-        hand_on(d, k)
+    def service_if(d, k):
+        @pl.when(t >= d)
+        def _():
+            service(d, k)
 
     loads[6].wait()
     loads[7].wait()
+    mix(0)
+    send_sums(2)
+    project(0)
+    send_cross(0)
+    mix(1)
+    project(1)
+    mix(2)
+    project(2)
     everything = slice(0, rows)
-    add_cache(me, everything, True)
-    add_query(me, everything, True)
-    arrivals = [gather.arrivals() for gather in vx_gathers]
-    for k in range(chunks):
-        slot = next(arrivals[k])
-    add_cache(slot, everything, False)
-    add_query(slot, everything, False)
     for k in range(chunks):
         span = chunk_slice(k)
+        add_cache(me, span, True)
+        if k == 0:
+            gathered = [gather.arrivals() for gather in vx_gathers]
+            near = next(gathered[0])
+        arrivals = gathered[k]
+        add_cache(near, span, False)
+        if k == 0:
+            send_cross(1)
         slots = []
-        for slot in arrivals[k]:
-            add_cache(slot, span, False)
-            slots.append(slot)
+        for d in range(1, chips):
+            slots.append(next(arrivals))
+            add_cache(slots[-1], span, False)
+            if k > 0:
+                add_query(slots[-1], span, False)
+            for due in range(min(k, spans - 1) if d == 1 else 0):
+                service_if(k - due, due)
+            slots.append(next(arrivals))
+            add_cache(slots[-1], span, False)
+            if k > 0 and d < chips - 1:
+                add_query(slots[-1], span, False)
         finish_cache(k)
-        hand_on(0, k)
-        for slot in slots:
-            add_query(slot, span, False)
+        hand_on(k)
+        if k == 0:
+            for others in gathered[1:]:
+                next(others)
+            add_query(me, everything, True)
+            add_query(near, everything, False)
+            for slot in slots:
+                add_query(slot, span, False)
+        else:
+            add_query(slots[-1], span, False)
         finish_query(k)
-        for d in range(1, min(k, spans - 1) + 1):
-
-            @pl.when(t >= d)
-            def _(d=d, k=k):
-                service(d, k - d)
+        if k == 0:
+            send_cross(2)
+    def attend(first, blocks, span, diagonal):
+        length = blocks * (span.stop - span.start)
+
+        beside = 3 if q_heads % 3 == 0 else 1
+
+        @pl.loop(0, q_heads // beside)
+        def _(n):
+            heads = [n * beside + i for i in range(beside)]
+            groups_of = [(me * q_heads + i) // GROUP for i in heads]
+            old = [(peak[i], denom[i], numer[i]) for i in heads]
+
+            def block(head):
+                cols = pl.ds(pl.multiple_of(lax.rem(head, ch) * HD, HD), HD)
+                return kv[pl.ds(first, blocks), head // ch, span, cols].reshape(length, HD)
+
+            scores = [
+                lax.dot_general(block(g), qs[i], (((1,), (1,)), ((), ())), preferred_element_type=F32)
+                for i, g in zip(heads, groups_of)
+            ]
+            if diagonal:
+                k_pos = lax.broadcasted_iota(jnp.int32, (length, rows), 0)
+                q_pos = lax.broadcasted_iota(jnp.int32, (length, rows), 1)
+                scores = [jnp.where(k_pos <= q_pos, x, masked) for x in scores]
+            tops = [jnp.maximum(o[0], jnp.max(x, axis=0, keepdims=True)) for o, x in zip(old, scores)]
+            weights = [jnp.exp2(x - top) for x, top in zip(scores, tops)]
+            products = [
+                lax.dot_general(
+                    block(KVH + g), w.astype(BF), (((0,), (0,)), ((), ())), preferred_element_type=F32
+                )
+                for g, w in zip(groups_of, weights)
+            ]
+            added = [jnp.sum(w, axis=0, keepdims=True) for w in weights]
+            for i, o, top, plus, product in zip(heads, old, tops, added, products):
+                rescale = jnp.exp2(o[0] - top)
+                peak[i] = top
+                denom[i] = o[1] * rescale + plus
+                numer[i] = o[2] * rescale + product
+
+    most = min(3, spans - 1)
+
+    def attend_earlier(span):
+        @pl.loop(0, t // most)
+        def _(n):
+            attend(n * most, most, span, False)
+
+        for left in range(1, most):
+
+            @pl.when(lax.rem(t, most) == left)
+            def _(left=left):
+                attend(t - left, left, span, False)
 
     def wave(w):
         for k in range(chunks):
@@ -558,69 +668,36 @@
             def _(d=d, k=k):
                 service(d, k)
 
-    def attend(d, diagonal):
-        j = lax.rem(t + spans - d, spans)
-
-        @pl.loop(0, q_heads, unroll=3 if q_heads % 3 == 0 else 1)
-        def _(i):
-            g = (me * q_heads + i) // GROUP
-            k_cols = pl.ds(pl.multiple_of(lax.rem(g, ch) * HD, HD), HD)
-            keys = kv[j, g // ch, :, k_cols]
-            values = kv[j, (KVH + g) // ch, :, pl.ds(pl.multiple_of(lax.rem(KVH + g, ch) * HD, HD), HD)]
-            scores = lax.dot_general(
-                qs[i], keys, (((1,), (1,)), ((), ())), preferred_element_type=F32
-            ) * (HD ** -0.5 * 1.4426950408889634)
-            if diagonal:
-                q_pos = lax.broadcasted_iota(jnp.int32, (rows, rows), 0)
-                k_pos = lax.broadcasted_iota(jnp.int32, (rows, rows), 1)
-                scores = jnp.where(k_pos <= q_pos, scores, masked)
-            top = jnp.max(scores, axis=1, keepdims=True)
-            if diagonal:
-                new_peak = jnp.broadcast_to(top, (rows, HD))
-            else:
-                new_peak = jnp.maximum(peak[i], top)
-            weights = jnp.exp2(scores - new_peak[:, 0:1])
-            added = jnp.sum(weights, axis=1, keepdims=True)
-            product = jnp.dot(weights.astype(BF), values, preferred_element_type=F32)
-            if diagonal:
-                denom[i] = jnp.broadcast_to(added, (rows, HD))
-                numer[i] = product
-            else:
-                rescale = jnp.exp2(peak[i] - new_peak)
-                denom[i] = denom[i] * rescale + added
-                numer[i] = numer[i] * rescale + product
-            peak[i] = new_peak
-
-    def share_wait_all(d):
-        for k in range(chunks):
-            share_wait(d, k)
-
-    last = t == spans - 1
-
-    @pl.when(t < spans - 1)
-    def _():
-        @pl.loop(chunks, chunks + t)
-        def _(w):
-            wave(w)
-
-    @pl.when(last & (t > 0))
-    def _():
-        wave(chunks)
-
-    share_wait_all(0)
-    attend(0, True)
+    wave(chunks)
+    share_wait(0, 0)
+    share_wait(0, 1)
+    attend(t, 1, everything, True)
+
+    @pl.loop(chunks + 1, chunks + t)
+    def _(w):
+        wave(w)
+
 
     @pl.loop(1, t + 1)
     def _(d):
-        @pl.when(last & (d < t))
-        def _():
-            wave(chunks + d)
-
-        share_wait_all(d)
-        attend(d, False)
+        share_wait(d, 0)
+
+    attend_earlier(slice(0, plan[2][0]))
+
+    @pl.loop(1, t + 1)
+    def _(d):
+        share_wait(d, 1)
+
+    attend_earlier(slice(plan[2][0], rows))
 
     for i in range(q_heads):
-        attention[:, i * HD : (i + 1) * HD] = (numer[i] / denom[i]).astype(BF)
+        attention[:, i * HD : (i + 1) * HD] = (numer[i] / denom[i]).T.astype(BF)
+    outs = [
+        pltpu.make_async_copy(attention, attention_out, out_sem.at[0]),
+        pltpu.make_async_copy(key_value, key_value_out, out_sem.at[1]),
+    ]
+    outs[0].start()
+    outs[1].start()
 
 
     @pl.when(t < spans - 1)
@@ -628,10 +705,12 @@
         for copy in up:
             copy.wait_send()
 
+    @pl.when(t < spans - 1)
+    def _():
         @pl.loop(0, t + 1)
         def _(d):
-            for k in range(chunks):
-                pass_copy(d, k).wait_send()
+            block = kv.at[lax.rem(t + spans - d, spans), me]
+            remote(block, block, z_ss.at[d + 1], z_rs.at[d + 1, 0], {"tm": (t + 1) % spans}).wait_send()
 
     @pl.when(t > 0)
     def _():
@@ -640,17 +719,18 @@
 
     @pl.loop(0, t + 1)
     def _(d):
-        for k in range(chunks):
-            share_drain(d, k)
+        share_drain(d)
 
     wo_gather.drain()
-    for gather in vx_gathers:
-        gather.drain()
+    for k, gather in enumerate(vx_gathers):
+        for copy in gather.near + ([] if k < chunks - 1 else gather.cross[1:]):
+            copy.wait_send()
     for copy in rs + ab_copies + sq:
         copy.wait_send()
-    for copies in exchange:
-        for copy in copies:
-            copy.wait_send()
+    for copy in exchange[-1]:
+        copy.wait_send()
+    for copy in outs:
+        copy.wait()
 
 
 def rows_first(x):
@@ -680,9 +760,9 @@
     frames_here, patches_here, width = features.shape
     cells = frames_here * patches_here
     rows = queries.shape[0]
-    chunks = max(1, rows // chunk_rows)
-    size = rows // chunks
-    part = size // 2
+    plan = row_chunks(rows)
+    chunks = len(plan)
+    padded = max(-(-size // HD) * HD for _, size in plan)
     frequency = rope_base ** (-2.0 * np.arange(HD // 2, dtype=np.float64) / HD)
     sign = np.concatenate([-np.ones(HD // 2), np.ones(HD // 2)])
 
@@ -697,20 +777,25 @@
     c_width = cache_weight.shape[1]
     q_heads = q_width // HD
     chips = groups // 2
+    table = shared_heads(groups, q_heads, c_width // HD)
+    most_sent = 1 + max(entry[4] for entry in table)
+    most_received = 1 + max(entry[5] for entry in table)
     vmem = pl.BlockSpec(memory_space=pltpu.VMEM)
     hbm = pl.BlockSpec(memory_space=pltpu.HBM)
     dma = pltpu.SemaphoreType.DMA
     V = pltpu.VMEM
     return tuple(
         pl.pallas_call(
-            functools.partial(kernel, groups, spans, frames_here, chunks),
+            functools.partial(kernel, groups, spans, frames_here, plan),
             out_shape=(
                 jax.ShapeDtypeStruct((rows, q_width), BF),
                 jax.ShapeDtypeStruct((rows, c_width), BF),
             ),
             in_specs=[hbm] * 3 + [vmem] * 10 + [hbm] * 5,
-            out_specs=(vmem, vmem),
+            out_specs=(pl.BlockSpec(memory_space=pl.ANY),) * 2,
             scratch_shapes=[
+                V((rows, q_width), BF),
+                V((rows, c_width), BF),
                 V((cells, width), BF),
                 V((rows, width), BF),
                 V((2, rows, HD), F32),
@@ -729,36 +814,37 @@
                 V((width, width), BF),
                 V((width, rows), F32),
                 V((rows, width), F32),
-                V((chunks, part, width), BF),
-                V((chunks, part, width), BF),
-                V((chips, chunks, part, width), BF),
-                V((chunks, 2, part, width), BF),
+                V((rows // 2, width), BF),
+                V((rows // 2, width), BF),
+                V((chips, rows // 2, width), BF),
+                V((rows, width), BF),
                 V((groups, rows, model), BF),
-                V((chunks, groups, 8, -(-size // HD) * HD), F32),
+                V((chunks, groups, 8, padded), F32),
                 V((rows, HD), F32),
                 V((rows, q_width), F32),
                 V((rows, c_width), F32),
                 V((q_heads, rows, HD), BF),
                 V((spans, groups, rows, c_width), BF),
-                V((q_heads, rows, HD), F32),
-                V((q_heads, rows, HD), F32),
-                V((q_heads, rows, HD), F32),
+                V((q_heads, 1, rows), F32),
+                V((q_heads, 1, rows), F32),
+                V((q_heads, HD, rows), F32),
                 dma((8,)),
+                dma((2,)),
                 dma((2, 2)),
                 dma((2, 2)),
                 dma((chunks,)),
                 dma((chunks,)),
-                dma((chunks, chips)),
-                dma((chunks, chips)),
+                dma((chunks, chips - 1)),
+                dma((chunks, chips - 1)),
                 dma((chunks,)),
                 dma((chunks,)),
-                dma((chunks, groups)),
-                dma((chunks, groups)),
+                dma((chunks,)),
+                dma((chunks,)),
+                dma((spans,)),
                 dma((spans, chunks)),
-                dma((spans, chunks)),
-                dma((spans, chunks, groups)),
-                dma((spans, chunks, groups)),
-                dma((1 + chunks, 4, chips)),
+                dma((spans, most_sent)),
+                dma((spans, 2, most_received)),
+                dma((1 + chunks, 4 * chips - 2)),
             ],
             compiler_params=pltpu.CompilerParams(
                 collective_id=0, has_side_effects=True, vmem_limit_bytes=48 * 1024 * 1024

time: 64.5 us -> 60.2 us (0.933)
  Pallas kernels: 62.3 us -> 57.9 us
    pallas_call x1, Pallas kernels: 62.3 us -> 57.9 us  [local(): pl.pallas_call(functools.partial(kernel, groups, spans, frames_here, plan...]
where the time goes in v4:
time: 60.2 us; the launch traced here: 60 us
  Pallas kernels  57.9 us (96%)
  local copies, waits for them, and re-layouts  1.4 us (2%)
  between operations  0.65 us (1%)
    pallas_call x1, Pallas kernels, local(): pl.pallas_call(functools.partial(kernel, groups, spans, frames_here, plan...  57.9 us
    unnamed x2, local copies, waits for them, and re-layouts  1.4 us

profile of v4, /device:TPU:27, one launch (start us, length us, event | category | flops | bytes accessed | tf_op | source)
XLA Modules:
  0.0 60.0 jit_solution(9316358429819264219)
XLA Ops:
  0.6 57.9 %shard_map.185 = (bf16[256,768]{1,0:T(8,128)(2,1)S(1)}, bf16[256,256]{1,0:T(8,128)(2,1)S(1)}) custom-call(bf16[576,1024]{1,0:T(8,128)(2,1)} %bitcast.10, bf16[256,1024]{1,0:T(8,128)(2,1)} %queries_hbm.1, f32[2,256,128]{2,1,0:T(8,128)} %constant.4.clone.row_turn_hbm, s32[1,256]{1,0:T(1,128)} %bitcast.16, s32[1,256]{1,0:T(1,128)} %bitcast.17, ...), custom_call_target="tpu_custom_call" | custom-call | tf_op jit(solution)/shard_map/pallas_call | solution.py:788
  58.6 0.7 %copy.22 = bf16[256,768]{1,0:T(8,128)(2,1)} copy(bf16[256,768]{1,0:T(8,128)(2,1)S(1)} %get-tuple-element.4) | data formatting | bytes 786432
  59.3 0.7 %copy.23 = bf16[256,256]{1,0:T(8,128)(2,1)} copy(bf16[256,256]{1,0:T(8,128)(2,1)S(1)} %get-tuple-element.5) | data formatting | bytes 262144
